TPU v7x, 32 devices: a whole 2x2x4 slice. The times are simulated.
32 devices in a mesh: rep: 1, dp: 32 (over x, y, z, core).
Axes of the slice: x: 2, y: 2, z: 4, core: 2. Of those that a mesh axis runs over, the one named last changes fastest.
Arguments:
- x: bfloat16 [32, 2048, 896], P(('rep', 'dp'))
- dy: bfloat16 [32, 2048, 896], P(('rep', 'dp'))
- w_gate: bfloat16 [2, 896, 2304], P(None, 'dp')
- w_up: bfloat16 [2, 896, 2304], P(None, 'dp')
- w_down: bfloat16 [2, 2304, 896], P(None, 'dp')
Outputs:
- output 1: bfloat16 [32, 2048, 896], P(('rep', 'dp'))
- output 2: bfloat16 [2, 896, 2304], P('rep', 'dp')
- output 3: bfloat16 [2, 896, 2304], P('rep', 'dp')
- output 4: bfloat16 [2, 2304, 896], P('rep', 'dp')
All inputs are finite; a program needn't handle non-finite values.
Results may differ from a plain program's by a relative error of at most 0.018.
Values are sent between devices in bfloat16 or wider.
A program may use at most 2 GiB of HBM per device.

v0:
```python
import jax
import jax.numpy as jnp
from jax import lax

NAMES = ("w_gate", "w_up", "w_down")


def matmul(a, w):
    return jnp.dot(a, w, preferred_element_type=jnp.float32).astype(jnp.bfloat16)


def normed(h):
    wide = h.astype(jnp.float32)
    scale = lax.rsqrt(jnp.mean(wide**2, -1, keepdims=True) + 1e-6)
    return (wide * scale).astype(jnp.bfloat16)


def layer(h, w):
    a = normed(h)
    gate = jnp.dot(a, w["w_gate"], preferred_element_type=jnp.float32)
    up = jnp.dot(a, w["w_up"], preferred_element_type=jnp.float32)
    return h + matmul((jax.nn.silu(gate) * up).astype(jnp.bfloat16), w["w_down"])


def stack(weights, h):
    for number in range(weights["w_gate"].shape[0]):
        h = layer(h, {name: w[number] for name, w in weights.items()})
    return h


def solution(mesh):
    groups = mesh.shape["rep"]

    def step(x, dy, *weights):
        shape = x.shape
        x, dy = (t.reshape(groups, -1, *t.shape[1:]) for t in (x, dy))

        def of_a_group(x, dy):
            _, back = jax.vjp(stack, dict(zip(NAMES, weights, strict=True)), x)
            by_weights, by_x = back(dy)
            return (by_x, *(by_weights[name] for name in NAMES))

        by_x, *by_weights = jax.vmap(of_a_group)(x, dy)
        return (by_x.reshape(shape), *(t.reshape(-1, *t.shape[2:]) for t in by_weights))

    return step
```

profile of v0, /device:TPU:0, one launch (start us, length us, event | category | flops | bytes accessed | tf_op | source)
XLA Modules:
  0.0 1847.4 jit_solution(594974361093688916)
XLA Ops:
  14.9 6.2 copy.23
  28.9 6.1 copy.25
  39.9 206.1 %while.13 = (bf16[1,2048,896]{2,1,0:T(8,128)(2,1)}, bf16[1,72,896]{2,1,0:T(8,128)(2,1)S(1)}, bf16[1,2048,2304]{1,2,0:T(8,128)(2,1)}, bf16[1,72,896]{2,1,0:T(8,12...) while((bf16[1,2048,896]{2,1,0:T(8,128)(2,1)}, ...), condition=%wide.windowed_dot_general_cond_ag, body=%wide.windowed_dot_general_body_ag.sunk | while | flops 1057222656 | bytes 13459997 | solution.py:9
  39.9 6.4 collective-permute-start
  51.4 6.0 collective-permute-done.2
  168.9 6.2 collective-permute-done.3
  216.4 5.8 collective-permute-done.3
  246.1 12.7 copy.24
  258.8 17.7 fusion.203
  276.5 25.3 %fusion.176 = (bf16[1,2048,2304]{2,1,0:T(8,128)(2,1)}, f32[2048,2304]{1,0:T(8,128)}) fusion(f32[2048,2304]{1,0:T(8,128)} %fusion.203, bf16[1,896,2304]{2,0,1:T(2,128)(2,1)} %all-gather.29.cloned.1.call-done, bf16[1,2048,896]{1,2,0:T(8,128)(2,1)} %fusion.188), kind=kOutput, calls=%fused_computation.215 | convolution fusion | flops 8484028416 | bytes 54984704 | tf_op jit(solution)/vmap(jvp())/dot_general | solution.py:21
  301.8 12.2 copy.28
  314.0 13.8 fusion.190
  332.4 17.7 fusion.197
  350.1 56.1 %all-gather.35.cloned.1.call-done = bf16[1,896,2304]{2,0,1:T(2,128)(2,1)} async-done(((bf16[1,28,2304]{2,0,1:T(2,128)(2,1)}), bf16[1,896,2304]{2,0,1:T(2,128)(2,1)}) %all-gather.35.cloned.1.call-update) | async-done | bytes 4128784 | tf_op jit(solution)/vmap(jvp())/squeeze | solution.py:27
  406.2 25.3 %fusion.170 = (bf16[1,2048,2304]{2,1,0:T(8,128)(2,1)}, f32[2048,2304]{1,0:T(8,128)}) fusion(f32[2048,2304]{1,0:T(8,128)} %fusion.197, bf16[1,896,2304]{2,0,1:T(2,128)(2,1)} %all-gather.35.cloned.1.call-done, bf16[1,2048,896]{1,2,0:T(8,128)(2,1)} %fusion.191), kind=kOutput, calls=%fused_computation.205 | convolution fusion | flops 8484028416 | bytes 54984704 | tf_op jit(solution)/vmap(jvp())/dot_general | solution.py:21
  431.5 12.8 copy.26
  444.3 196.6 %while.18 = (bf16[1,2048,2304]{1,2,0:T(8,128)(2,1)}, bf16[1,2048,896]{2,1,0:T(8,128)(2,1)}, f32[72,896]{1,0:T(8,128)S(1)}, f32[72,896]{1,0:T(8,128)}, u32[]{:T(1...) while((bf16[1,2048,2304]{1,2,0:T(8,128)(2,1)}, ...), condition=%wide.windowed_dot_general_cond_rs.4.clone, body=%wide.windowed_dot_general_body_rs.4.clone.sunk | while | flops 1059710976 | bytes 87933576 | solution.py:9
  536.4 5.8 collective-permute-done.22
  560.9 5.8 collective-permute-done.22
  585.4 5.8 collective-permute-done.22
  609.8 5.8 collective-permute-done.22
  634.3 5.8 collective-permute-done.22
  640.9 17.7 convert_multiply_fusion.3
  658.7 16.5 fusion.168
  675.2 15.0 fusion.192
  690.3 7.7 fusion.208
  697.9 6.0 copy.27
  704.0 195.8 %while.19 = (bf16[1,2048,896]{2,1,0:T(8,128)(2,1)}, bf16[1,2048,2304]{1,2,0:T(8,128)(2,1)}, f32[896,72]{0,1:T(8,128)S(1)}, f32[896,72]{0,1:T(8,128)}, u32[]{:T(1...) while((bf16[1,2048,896]{2,1,0:T(8,128)(2,1)}, ...), condition=%wide.windowed_dot_general_cond_rs.5.clone, body=%wide.windowed_dot_general_body_rs.5.clone.sunk | while | flops 1059710976 | bytes 78496440 | solution.py:9
  746.4 5.6 collective-permute-done.26
  770.9 5.9 collective-permute-done.26
  795.4 5.6 collective-permute-done.26
  819.9 5.9 collective-permute-done.26
  844.4 5.6 collective-permute-done.26
  868.9 5.9 collective-permute-done.26
  893.4 5.6 collective-permute-done.26
  900.5 215.5 %while.16 = (bf16[1,2048,2304]{2,1,0:T(8,128)(2,1)}, bf16[1,2048,896]{1,2,0:T(8,128)(2,1)}, f32[2304,28]{0,1:T(8,128)S(1)}, f32[2304,28]{0,1:T(8,128)}, u32[]{:T...) while((bf16[1,2048,2304]{2,1,0:T(8,128)(2,1)}, ...), condition=%wide.windowed_dot_general_cond_rs.2.clone, body=%wide.windowed_dot_general_body_rs.2.clone.sunk | while | flops 1058269184 | bytes 35504720 | solution.py:21
  906.0 5.6 fusion.331
  920.9 5.6 fusion.333
  947.1 5.6 fusion.333
  988.0 5.6 fusion.331
  1041.8 5.6 fusion.331
  1116.0 30.6 %convert_multiply_fusion.1 = (bf16[1,2048,2304]{2,1,0:T(8,128)(2,1)}, bf16[1,2048,2304]{2,1,0:T(8,128)(2,1)}) fusion(f32[2048,2304]{1,0:T(8,128)} %fusion.203, f32[2048,2304]{1,0:T(8,128)} %get-tuple-element.310, bf16[1,2304,896]{2,1,0:T(8,128)(2,1)} %all-gather.31.cloned.1.call-done, bf16[1,2048,896]{1,2,0:T(8,128)(2,1)} %fusion.208), kind=kOutput, calls=%fused_computation.191 | convolution fusion | flops 8531214336 | bytes 64421888 | tf_op jit(solution)/vmap(transpose(jvp()))/dot_general | solution.py:9
  1146.6 214.1 %while.17 = (bf16[1,2048,2304]{2,1,0:T(8,128)(2,1)}, bf16[1,2048,896]{1,2,0:T(8,128)(2,1)}, f32[2304,28]{0,1:T(8,128)S(1)}, f32[2304,28]{0,1:T(8,128)}, u32[]{:T...) while((bf16[1,2048,2304]{2,1,0:T(8,128)(2,1)}, ...), condition=%wide.windowed_dot_general_cond_rs.3.clone, body=%wide.windowed_dot_general_body_rs.3.clone.sunk | while | flops 1058269184 | bytes 35504720 | solution.py:21
  1152.2 5.6 fusion.339
  1205.9 5.6 fusion.339
  1218.7 5.6 fusion.341
  1232.8 5.6 fusion.339
  1272.5 5.6 fusion.341
  1286.5 5.6 fusion.339
  1326.2 5.6 fusion.341
  1361.4 208.0 %while.14 = (bf16[1,2048,2304]{2,1,0:T(8,128)(2,1)}, bf16[1,2048,896]{1,2,0:T(8,128)(2,1)}, f32[2304,28]{0,1:T(8,128)S(1)}, f32[2304,28]{0,1:T(8,128)S(1)}, u32[...) while((bf16[1,2048,2304]{2,1,0:T(8,128)(2,1)}, ...), condition=%wide.windowed_dot_general_cond_rs.clone, body=%wide.windowed_dot_general_body_rs.clone.sunk | while | flops 1058269184 | bytes 35504720 | solution.py:20
  1406.0 5.6 fusion.317
  1419.1 5.6 fusion.315
  1471.3 5.6 fusion.315
  1562.6 5.6 fusion.317
  1570.2 208.3 %while.15 = (bf16[1,2048,2304]{2,1,0:T(8,128)(2,1)}, bf16[1,2048,896]{1,2,0:T(8,128)(2,1)}, f32[2304,28]{0,1:T(8,128)S(1)}, f32[2304,28]{0,1:T(8,128)S(1)}, u32[...) while((bf16[1,2048,2304]{2,1,0:T(8,128)(2,1)}, ...), condition=%wide.windowed_dot_general_cond_rs.1.clone, body=%wide.windowed_dot_general_body_rs.1.clone.sunk | while | flops 1058269184 | bytes 35504720 | solution.py:20
  1588.5 5.6 fusion.325
  1653.8 5.6 fusion.323
  1732.0 5.6 fusion.323
  1778.6 16.5 fusion.164
  1795.2 14.6 fusion.189
  1809.8 6.6 fusion.207
  1816.4 6.2 copy.29
  1824.7 7.8 collective-permute-done.29
  (987 shorter events, 1278.2 us)
Async XLA Ops:
  7.2 251.6 %all-gather.27.cloned.1.call-start = ((), (), s32[]{:S(2)}) async-start(), calls=%async_computation | async-start | bytes 8515584 | tf_op jit(solution)/vmap(jvp())/squeeze | solution.py:27
  9.5 267.0 %all-gather.29.cloned.1.call-start = ((), (), s32[]{:S(2)}) async-start(), calls=%async_computation.1 | async-start | bytes 8515584 | tf_op jit(solution)/vmap(jvp())/squeeze | solution.py:27
  11.9 302.1 %all-gather.31.cloned.1.call-start = ((), (), s32[]{:S(2)}) async-start(), calls=%async_computation.2 | async-start | bytes 4257792 | tf_op jit(solution)/vmap(jvp())/squeeze | solution.py:27
  13.6 318.7 %all-gather.33.cloned.1.call-start = ((), (), s32[]{:S(2)}) async-start(), calls=%async_computation.3 | async-start | bytes 8515584 | tf_op jit(solution)/vmap(jvp())/squeeze | solution.py:27
  14.2 392.0 %all-gather.35.cloned.1.call-start = ((), (), s32[]{:S(2)}) async-start(), calls=%async_computation.4 | async-start | bytes 8515584 | tf_op jit(solution)/vmap(jvp())/squeeze | solution.py:27
  14.3 20.7 %collective-permute-start.28 = (bf16[1,72,896]{2,1,0:T(8,128)(2,1)S(1)}, bf16[1,72,896]{2,1,0:T(8,128)(2,1)S(1)}, u32[]{:S(2)}, u32[]{:S(2)}) collective-permute-start(bf16[1,72,896]{2,1,0:T(8,128)(2,1)S(1)} %get-tuple-element.585), channel_id=6, source_target_pairs={{0,1},{1,2},{2,3},{3,4},{4,5},{5,6},{6,7},{7,8},{8,9},{9,10},{10,1... | collective-permute-start | bytes 387080 | tf_op jit(solution)/vmap(transpose(jvp()))/dot_general | solution.py:9
  640.9 1196.8 %collective-permute-start.33 = (f32[72,896]{1,0:T(8,128)}, f32[72,896]{1,0:T(8,128)}, u32[]{:S(2)}, u32[]{:S(2)}) collective-permute-start(f32[72,896]{1,0:T(8,128)} %get-tuple-element.52), channel_id=46, source_target_pairs={{0,1},{1,2},{2,3},{3,4},{4,5},{5,6},{6,7},{7,8},{8,9},{9,10},{10,1... | collective-permute-start | bytes 774152 | tf_op jit(solution)/vmap(transpose(jvp()))/dot_general | solution.py:9
  899.8 938.9 %collective-permute-start.34 = (f32[896,72]{0,1:T(8,128)}, f32[896,72]{0,1:T(8,128)}, u32[]{:S(2)}, u32[]{:S(2)}) collective-permute-start(f32[896,72]{0,1:T(8,128)} %get-tuple-element.54), channel_id=52, source_target_pairs={{0,1},{1,2},{2,3},{3,4},{4,5},{5,6},{6,7},{7,8},{8,9},{9,10},{10,1... | collective-permute-start | bytes 774152 | tf_op jit(solution)/vmap(transpose(jvp()))/dot_general | solution.py:9
  900.5 15.0 collective-permute-start.12
  900.6 14.9 collective-permute-start.13
  928.8 12.7 collective-permute-start.12
  928.9 12.6 collective-permute-start.13
  955.6 12.6 collective-permute-start.12
  982.5 12.7 collective-permute-start.12
  982.6 12.6 collective-permute-start.13
  1009.4 12.6 collective-permute-start.12
  1036.3 12.7 collective-permute-start.12
  1036.4 12.6 collective-permute-start.13
  1063.2 12.6 collective-permute-start.12
  1090.1 12.7 collective-permute-start.12
  1090.2 12.6 collective-permute-start.13
  1116.0 706.6 %collective-permute-start.31 = (f32[2304,28]{0,1:T(8,128)}, f32[2304,28]{0,1:T(8,128)}, u32[]{:S(2)}, u32[]{:S(2)}) collective-permute-start(f32[2304,28]{0,1:T(8,128)} %get-tuple-element.48), channel_id=34, source_target_pairs={{0,1},{1,2},{2,3},{3,4},{4,5},{5,6},{6,7},{7,8},{8,9},{9,10},{10,1... | collective-permute-start | bytes 774152 | tf_op jit(solution)/vmap(transpose(jvp()))/dot_general | solution.py:21
  1173.6 12.7 collective-permute-start.16
  1173.7 12.6 collective-permute-start.17
  1227.3 12.7 collective-permute-start.16
  1227.4 12.6 collective-permute-start.17
  1254.2 12.6 collective-permute-start.16
  1281.1 12.7 collective-permute-start.16
  1281.2 12.6 collective-permute-start.17
  1307.9 12.6 collective-permute-start.16
  1334.8 12.7 collective-permute-start.16
  1334.9 12.6 collective-permute-start.17
  1361.7 12.6 collective-permute-start.4
  1374.4 12.8 collective-permute-start.7
  1387.4 12.9 collective-permute-start.5
  1400.5 12.9 collective-permute-start.7
  1413.5 12.9 collective-permute-start.5
  1426.5 12.9 collective-permute-start.7
  1439.6 12.9 collective-permute-start.5
  1452.6 12.9 collective-permute-start.7
  1465.7 12.9 collective-permute-start.5
  1478.7 12.9 collective-permute-start.7
  1491.8 12.9 collective-permute-start.5
  1504.8 12.9 collective-permute-start.7
  1517.9 12.9 collective-permute-start.5
  1530.9 12.9 collective-permute-start.7
  1544.0 12.9 collective-permute-start.5
  1582.9 12.9 collective-permute-start.11
  1596.0 12.9 collective-permute-start.9
  1609.0 12.9 collective-permute-start.11
  1622.1 12.9 collective-permute-start.9
  1635.1 12.9 collective-permute-start.11
  1648.2 12.9 collective-permute-start.9
  1661.2 12.9 collective-permute-start.11
  1674.3 12.9 collective-permute-start.9
  1687.3 12.9 collective-permute-start.11
  1700.4 12.9 collective-permute-start.9
  1713.4 12.9 collective-permute-start.11
  1726.4 12.9 collective-permute-start.9
  1739.5 12.9 collective-permute-start.11
  1752.5 12.9 collective-permute-start.9
  1765.6 12.8 collective-permute-start.11
  1778.5 45.2 %collective-permute-start.32 = (f32[2304,28]{0,1:T(8,128)}, f32[2304,28]{0,1:T(8,128)}, u32[]{:S(2)}, u32[]{:S(2)}) collective-permute-start(f32[2304,28]{0,1:T(8,128)} %get-tuple-element.50), channel_id=40, source_target_pairs={{0,1},{1,2},{2,3},{3,4},{4,5},{5,6},{6,7},{7,8},{8,9},{9,10},{10,1... | collective-permute-start | bytes 774152 | tf_op jit(solution)/vmap(transpose(jvp()))/dot_general | solution.py:21
  1822.6 13.1 collective-permute-start.30
  (255 other events, 3906.6 us)
Sparse Core Ops, SparseCore 0:
  11.6 83.1 all-gather.26
  97.8 84.3 all-gather.28
  185.1 62.2 all-gather.30
  250.9 76.3 all-gather.32
  330.7 75.4 all-gather.34
where the time goes:
time: 1860 us; the launch traced here: 1850 us
  matrix products  672 us (36%)
  starting transfers between devices  555 us (30%)
  waiting for transfers between devices  393 us (21%)
  other arithmetic  106 us (6%)
  local copies, waits for them, and re-layouts  103 us (6%)
    dot_general x36, matrix products, layer(): up = jnp.dot(a, w['w_up'], preferred_element_type=jnp.float32)  260 us
    dot_general x36, matrix products, layer(): gate = jnp.dot(a, w['w_gate'], preferred_element_type=jnp.float32)  248 us
    dot_general x99, waiting for transfers between devices, matmul(): jnp.dot(a, w, preferred_element_type=jnp.float32).astype(jnp.bfloat16)  227 us
    dot_general x99, starting transfers between devices, matmul(): jnp.dot(a, w, preferred_element_type=jnp.float32).astype(jnp.bfloat16)  199 us
    dot_general x66, starting transfers between devices, layer(): gate = jnp.dot(a, w['w_gate'], preferred_element_type=jnp.float32)  180 us
    dot_general x66, starting transfers between devices, layer(): up = jnp.dot(a, w['w_up'], preferred_element_type=jnp.float32)  176 us
    dot_general x50, matrix products, matmul(): jnp.dot(a, w, preferred_element_type=jnp.float32).astype(jnp.bfloat16)  165 us
    dot_general x66, waiting for transfers between devices, layer(): gate = jnp.dot(a, w['w_gate'], preferred_element_type=jnp.float32)  63.8 us
  transfers between devices with their start and end apart: 236, of which 156 were waited for; matrix products, arithmetic and copies ran while one was open for 44% of the time, Pallas kernels for 0%

commit v1 on v0

v1 whole, which is shorter than its diff:
```python
import jax
import jax.numpy as jnp
from jax import lax
from jax.sharding import PartitionSpec as P

EPS = 1e-6
F32, BF16 = jnp.float32, jnp.bfloat16


def dot(a, b, ca, cb):
    return lax.dot_general(a, b, (((ca,), (cb,)), ((), ())), preferred_element_type=F32)


def normed(h):
    wide = h.astype(F32)
    scale = lax.rsqrt(jnp.mean(wide**2, -1, keepdims=True) + EPS)
    return (wide * scale).astype(BF16)


def norm_back(h, by_a):
    wide, by_a = h.astype(F32), by_a.astype(F32)
    scale = lax.rsqrt(jnp.mean(wide**2, -1, keepdims=True) + EPS)
    return (scale * (by_a - wide * (scale * scale * jnp.mean(by_a * wide, -1, keepdims=True)))).astype(BF16)


def solution(mesh):
    devices = mesh.shape["dp"]

    def step(x, dy, w_gate, w_up, w_down):
        layers, rows, ff = w_gate.shape
        deep, d = w_down.shape[1:]
        size = rows * ff // 128
        parts = [t.reshape(layers, 1, size, 128) for t in (w_gate, w_up, w_down)]
        held = lax.all_gather(jnp.concatenate(parts, 1).reshape(layers * 3 * size, 128), "dp", axis=0)
        held = held.reshape(devices, layers, 3, size, 128)
        h, by_h = x[0], dy[0]
        kept = []
        for n in range(layers):
            wg, wu = (held[:, n, k].reshape(devices * rows, ff) for k in (0, 1))
            wd = held[:, n, 2].reshape(devices * deep, d)
            a = normed(h)
            gate, up = dot(a, wg, 1, 0), dot(a, wu, 1, 0)
            p = (jax.nn.silu(gate) * up).astype(BF16)
            kept.append((h, a, gate, up, p, wg, wu, wd))
            h = h + dot(p, wd, 1, 0).astype(BF16)
        by_weights = []
        for n in reversed(range(layers)):
            h, a, gate, up, p, wg, wu, wd = kept[n]
            by_p = dot(by_h, wd, 1, 1).astype(BF16).astype(F32)
            s = jax.nn.sigmoid(gate)
            by_up = (by_p * (gate * s)).astype(BF16)
            by_gate = (by_p * up * (s * (1 + gate * (1 - s)))).astype(BF16)
            terms = dot(a, by_gate, 0, 0), dot(a, by_up, 0, 0), dot(p, by_h, 0, 0)
            by_weights = [t.astype(BF16).reshape(devices, size, 128) for t in terms] + by_weights
            by_a = dot(by_gate, wg, 1, 1).astype(BF16) + dot(by_up, wu, 1, 1).astype(BF16)
            by_h = by_h + norm_back(h, by_a)
        sent = jnp.concatenate(by_weights, 1).reshape(-1, 128)
        own = lax.psum_scatter(sent, "dp", scatter_dimension=0, tiled=True).reshape(layers, 3, size, 128)
        return (by_h[None], *(own[:, k].reshape(w.shape) for k, w in enumerate((w_gate, w_up, w_down))))

    tokens, weights = P(("rep", "dp"), None, None), P(None, "dp", None)
    return jax.shard_map(
        step,
        mesh=mesh,
        in_specs=(tokens, tokens, weights, weights, weights),
        out_specs=(tokens, P("rep", "dp", None), P("rep", "dp", None), P("rep", "dp", None)),
        check_vma=False,
    )
```

time: 1860 us -> 823 us (0.44)
  starting transfers between devices: 555 us -> 0.08 us
  matrix products: 672 us -> 274 us
  other arithmetic: 106 us -> 14.4 us
  local copies, waits for them, and re-layouts: 103 us -> 168 us
  waiting for transfers between devices: 393 us -> 343 us
    dot_general x231 -> x0, starting transfers between devices: 555 us -> none  [the longest x99 199 us: matmul(): jnp.dot(a, w, preferred_element_type=jnp.float32).astype(jnp.bfloat16)]
    dot_general x122 -> x17, matrix products: 672 us -> 274 us  [dot(): lax.dot_general(a, b, (((ca,), (cb,)), ((), ())), preferred_element_type=...]
    dot_general x231 -> x0, waiting for transfers between devices: 336 us -> none  [the longest x99 227 us: matmul(): jnp.dot(a, w, preferred_element_type=jnp.float32).astype(jnp.bfloat16)]
    reduce_scatter x0 -> x1, waiting for transfers between devices: none -> 204 us  [step(): lax.psum_scatter(sent, 'dp', scatter_dimension=0, tiled=True)]
    all_gather x0 -> x1, waiting for transfers between devices: none -> 139 us  [step(): lax.all_gather(jnp.concatenate(parts, 1).reshape(layers * 3 * size, 128),...]
    dot_general x200 -> x0, other arithmetic: 58.4 us -> none
    squeeze x5 -> x0, waiting for transfers between devices: 56.1 us -> none  [stack(): h = layer(h, {name: w[number] for name, w in weights.items()})]
    reshape x0 -> x9, local copies, waits for them, and re-layouts: none -> 52.9 us  [the longest x6 51 us: step(): t.astype(BF16).reshape(devices, size, 128)]
  transfers between devices with their start and end apart: 236 -> 2, of which waited for: 156 -> 2; matrix products, arithmetic and copies ran while one was open for 44% -> 6% of each run, Pallas kernels for 0% -> 0%
where the time goes in v1:
time: 823 us; the launch traced here: 813 us
  waiting for transfers between devices  343 us (42%)
  matrix products  274 us (33%)
  local copies, waits for them, and re-layouts  168 us (20%)
  between operations  14.6 us (2%)
  other arithmetic  14.4 us (2%)
    dot_general x17, matrix products, dot(): lax.dot_general(a, b, (((ca,), (cb,)), ((), ())), preferred_element_type=...  274 us
    reduce_scatter x1, waiting for transfers between devices, step(): lax.psum_scatter(sent, 'dp', scatter_dimension=0, tiled=True)  204 us
    all_gather x1, waiting for transfers between devices, step(): lax.all_gather(jnp.concatenate(parts, 1).reshape(layers * 3 * size, 128),...  139 us
    reshape x6, local copies, waits for them, and re-layouts, step(): t.astype(BF16).reshape(devices, size, 128)  51 us
    unnamed x62, local copies, waits for them, and re-layouts  38.8 us
    another operation x4, local copies, waits for them, and re-layouts, step(): wg, wu = (held[:, n, k].reshape(devices * rows, ff) for k in (0, 1))  33.9 us
    slice x1, local copies, waits for them, and re-layouts, step(): wg, wu = (held[:, n, k].reshape(devices * rows, ff) for k in (0, 1))  18.9 us
    another operation x2, local copies, waits for them, and re-layouts, step(): wd = held[:, n, 2].reshape(devices * deep, d)  16.6 us
  transfers between devices with their start and end apart: 2, of which 2 were waited for; matrix products, arithmetic and copies ran while one was open for 6% of the time, Pallas kernels for 0%

profile of v1, /device:TPU:0, one launch (start us, length us, event | category | flops | bytes accessed | tf_op | source)
XLA Modules:
  0.0 812.9 jit_solution(11374081662347990886)
XLA Ops:
  7.2 0.0 all-gather.2.cloned.1.call-start
  7.2 1.2 reshape.98
  8.4 1.0 copy.24
  9.4 0.3 reshape.96
  9.7 1.0 copy.25
  10.7 0.3 reshape.97
  11.1 0.1 pad_maximum_fusion
  11.2 1.0 copy.26
  12.1 0.0 all-gather.2.cloned.1.call-update
  12.2 0.0 reduce-scatter.2.cloned.1.call-start
  12.2 6.1 copy.23
  18.3 6.1 copy.22
  24.4 2.8 fusion.13
  27.2 0.6 copy-done.15
  27.8 138.8 %all-gather.2.cloned.1.call-done = bf16[32,3024,128]{2,1,0:T(8,128)(2,1)} async-done(((bf16[1,3024,128]{2,1,0:T(8,128)(2,1)}), bf16[32,3024,128]{2,1,0:T(8,128)(2,1)}) %all-gather.2.cloned.1.call-update) | async-done | bytes 24772624 | tf_op jit(solution)/shard_map/all_gather | solution.py:34
  166.6 18.9 %fusion.40 = (bf16[32,1,1,504,128]{4,3,2,1,0:T(8,128)(2,1)}, bf16[32,1,1,504,128]{4,3,2,1,0:T(8,128)(2,1)}, bf16[32,1,1,504,128]{4,3,2,1,0:T(8,128)(2,1)}, bf16[...) fusion(bf16[32,2,3,504,128]{4,3,2,1,0:T(8,128)(2,1)} %bitcast.80), kind=kLoop, calls=%fused_computation.71 | loop fusion | bytes 49545216 | tf_op jit(solution)/shard_map/slice | solution.py:39
  185.5 8.5 %reshape_squeeze.32 = bf16[896,2304]{1,0:T(8,128)(2,1)} reshape(bf16[32,1,1,504,128]{4,3,2,1,0:T(8,128)(2,1)} %get-tuple-element.20) | data formatting | bytes 8257536 | tf_op jit(solution)/shard_map/reshape;squeeze | solution.py:39
  194.0 8.4 %reshape_squeeze.31 = bf16[896,2304]{1,0:T(8,128)(2,1)} reshape(bf16[32,1,1,504,128]{4,3,2,1,0:T(8,128)(2,1)} %get-tuple-element.21) | data formatting | bytes 8257536 | tf_op jit(solution)/shard_map/reshape;squeeze | solution.py:39
  202.5 8.3 %reshape_squeeze.29 = bf16[2304,896]{1,0:T(8,128)(2,1)} reshape(bf16[32,1,1,504,128]{4,3,2,1,0:T(8,128)(2,1)} %get-tuple-element.23) | data formatting | bytes 8257536 | tf_op jit(solution)/shard_map/reshape;squeeze | solution.py:40
  210.8 8.5 %reshape_squeeze.28 = bf16[896,2304]{1,0:T(8,128)(2,1)} reshape(bf16[32,1,1,504,128]{4,3,2,1,0:T(8,128)(2,1)} %get-tuple-element.24) | data formatting | bytes 8257536 | tf_op jit(solution)/shard_map/reshape;squeeze | solution.py:39
  219.3 8.5 %reshape_squeeze.27 = bf16[896,2304]{1,0:T(8,128)(2,1)} reshape(bf16[32,1,1,504,128]{4,3,2,1,0:T(8,128)(2,1)} %get-tuple-element.25) | data formatting | bytes 8257536 | tf_op jit(solution)/shard_map/reshape;squeeze | solution.py:39
  227.7 8.3 %reshape_squeeze.30 = bf16[2304,896]{1,0:T(8,128)(2,1)} reshape(bf16[32,1,1,504,128]{4,3,2,1,0:T(8,128)(2,1)} %get-tuple-element.22) | data formatting | bytes 8257536 | tf_op jit(solution)/shard_map/reshape;squeeze | solution.py:40
  236.0 17.1 %fusion.37 = f32[2048,2304]{1,0:T(8,128)} fusion(bf16[896,2304]{1,0:T(8,128)(2,1)} %reshape_squeeze.27, bf16[1,2048,896]{2,1,0:T(8,128)(2,1)} %param.5, f32[2048]{0:T(1024)S(1)} %add_rsqrt_fusion.1), kind=kOutput, calls=%fused_computation.58 | convolution fusion | flops 8461221888 | bytes 26681344 | tf_op jit(solution)/shard_map/dot_general | solution.py:11
  253.1 21.3 %multiply_convert_fusion.1 = (bf16[2048,2304]{1,0:T(8,128)(2,1)}, f32[2048,2304]{1,0:T(8,128)}) fusion(f32[2048,2304]{1,0:T(8,128)} %fusion.37, bf16[896,2304]{1,0:T(8,128)(2,1)} %reshape_squeeze.28, bf16[1,2048,896]{2,1,0:T(8,128)(2,1)} %param.5, f32[2048]{0:T(1024)S(1)} %add_rsqrt_fusion.1), kind=kOutput, calls=%fused_computation.13 | convolution fusion | flops 8489533440 | bytes 54992896 | tf_op jit(solution)/shard_map/dot_general | solution.py:11
  274.4 13.9 %fusion.16 = (f32[2048]{0:T(1024)S(1)}, bf16[2048,896]{0,1:T(8,128)(2,1)S(1)}) fusion(bf16[2048,2304]{1,0:T(8,128)(2,1)} %get-tuple-element.29, bf16[2304,896]{1,0:T(8,128)(2,1)} %reshape_squeeze.29, bf16[1,2048,896]{1,2,0:T(8,128)(2,1)} %copy.23), kind=kOutput, calls=%fused_computation.36 | convolution fusion | flops 8464889856 | bytes 20914176 | tf_op jit(solution)/shard_map/dot_general | solution.py:11
  288.4 0.0 copy-start.19
  288.4 13.5 %fusion.31 = f32[2048,2304]{1,0:T(8,128)} fusion(bf16[896,2304]{1,0:T(8,128)(2,1)S(1)} %copy-done.12, bf16[2048,896]{0,1:T(8,128)(2,1)S(1)} %get-tuple-element.32, f32[2048]{0:T(1024)S(1)} %add_rsqrt_fusion), kind=kOutput, calls=%fused_computation.55 | convolution fusion | flops 8461221888 | bytes 26681344 | tf_op jit(solution)/shard_map/dot_general | solution.py:11
  301.9 13.8 %fusion.33 = f32[2048,2304]{1,0:T(8,128)} fusion(bf16[896,2304]{1,0:T(8,128)(2,1)S(1)} %copy-done.10, bf16[2048,896]{0,1:T(8,128)(2,1)S(1)} %get-tuple-element.32, f32[2048]{0:T(1024)S(1)} %add_rsqrt_fusion), kind=kOutput, calls=%fused_computation.56 | convolution fusion | flops 8461221888 | bytes 26681344 | tf_op jit(solution)/shard_map/dot_general | solution.py:11
  315.6 19.5 %fusion.19 = bf16[2304,896]{1,0:T(8,128)(2,1)} fusion(f32[2048,2304]{1,0:T(8,128)} %fusion.33, bf16[1,2048,896]{2,1,0:T(8,128)(2,1)} %param.6, f32[2048,2304]{1,0:T(8,128)} %fusion.31), kind=kOutput, calls=%fused_computation.44 | convolution fusion | flops 8486092800 | bytes 45547520 | tf_op jit(solution)/shard_map/dot_general | solution.py:11
  335.1 31.4 %fusion.5 = (bf16[2048,2304]{1,0:T(8,128)(2,1)}, bf16[2048,2304]{1,0:T(8,128)(2,1)}) fusion(f32[2048,2304]{1,0:T(8,128)} %fusion.31, f32[2048,2304]{1,0:T(8,128)} %fusion.33, bf16[2304,896]{1,0:T(8,128)(2,1)} %reshape_squeeze.30, bf16[1,2048,896]{2,1,0:T(8,128)(2,1)} %param.6), kind=kOutput, calls=%fused_computation.9 | convolution fusion | flops 8526495744 | bytes 64421888 | tf_op jit(solution)/shard_map/dot_general | solution.py:11
  366.6 12.7 %fusion.42 = bf16[2048,896]{0,1:T(8,128)(2,1)S(1)} fusion(bf16[2048,2304]{1,0:T(8,128)(2,1)} %get-tuple-element.19, bf16[896,2304]{1,0:T(8,128)(2,1)} %reshape_squeeze.32), kind=kOutput, calls=%fused_computation.73 | convolution fusion | flops 8455716864 | bytes 17235968 | tf_op jit(solution)/shard_map/dot_general | solution.py:11
  379.3 13.6 %convolution_convert_fusion.3 = bf16[896,2304]{1,0:T(8,128)(2,1)} fusion(bf16[2048,2304]{1,0:T(8,128)(2,1)} %get-tuple-element.19, bf16[2048,896]{0,1:T(8,128)(2,1)S(1)} %copy-done.14, f32[2048]{0:T(1024)S(1)} %add_rsqrt_fusion), kind=kOutput, calls=%fused_computation.41 | convolution fusion | flops 8463286272 | bytes 17244160 | tf_op jit(solution)/shard_map/dot_general | solution.py:11
  392.9 10.5 %convolution_convert_fusion.2 = bf16[896,2304]{1,0:T(8,128)(2,1)} fusion(bf16[2048,2304]{1,0:T(8,128)(2,1)S(1)} %bitcast.84, bf16[2048,896]{0,1:T(8,128)(2,1)S(1)} %copy-done.14, f32[2048]{0:T(1024)S(1)} %add_rsqrt_fusion), kind=kOutput, calls=%fused_computation.40 | convolution fusion | flops 8463286272 | bytes 17244160 | tf_op jit(solution)/shard_map/dot_general | solution.py:11
  403.4 10.5 %fusion.18 = (f32[2048]{0:T(1024)S(1)}, bf16[2048,896]{0,1:T(8,128)(2,1)}) fusion(bf16[2048,896]{0,1:T(8,128)(2,1)S(1)} %copy-done.14, bf16[2048,896]{0,1:T(8,128)(2,1)S(1)} %fusion.42, bf16[2048,2304]{1,0:T(8,128)(2,1)S(1)} %bitcast.84, bf16[896,2304]{1,0:T(8,128)(2,1)S(1)} %copy-done.11), kind=kOutput, calls=%fused_computation.38 | convolution fusion | flops 8466724864 | bytes 24584192 | tf_op jit(solution)/shard_map/dot_general | solution.py:11
  413.9 8.6 %reshape.104 = bf16[32,504,128]{2,1,0:T(8,128)(2,1)} reshape(bf16[896,2304]{1,0:T(8,128)(2,1)} %convolution_convert_fusion.2) | data formatting | bytes 8257536 | tf_op jit(solution)/shard_map/reshape | solution.py:54
  422.5 8.6 %reshape.103 = bf16[32,504,128]{2,1,0:T(8,128)(2,1)} reshape(bf16[896,2304]{1,0:T(8,128)(2,1)} %convolution_convert_fusion.3) | data formatting | bytes 8257536 | tf_op jit(solution)/shard_map/reshape | solution.py:54
  431.1 6.9 fusion.23
  438.0 15.3 %convolution_convert_fusion.6 = bf16[2304,896]{1,0:T(8,128)(2,1)} fusion(bf16[2048,2304]{1,0:T(8,128)(2,1)} %get-tuple-element.29, bf16[2048,896]{0,1:T(8,128)(2,1)S(1)} %fusion.23), kind=kOutput, calls=%fused_computation.45 | convolution fusion | flops 8457781248 | bytes 17235968 | tf_op jit(solution)/shard_map/dot_general | solution.py:11
  453.3 30.7 %fusion.2 = (bf16[2048,2304]{1,0:T(8,128)(2,1)}, bf16[2048,2304]{1,0:T(8,128)(2,1)}) fusion(f32[2048,2304]{1,0:T(8,128)} %fusion.37, f32[2048,2304]{1,0:T(8,128)} %get-tuple-element.30, bf16[2048,896]{0,1:T(8,128)(2,1)} %copy-done.7, bf16[2304,896]{1,0:T(8,128)(2,1)} %reshape_squeeze.29), kind=kOutput, calls=%fused_computation.4 | convolution fusion | flops 8526495744 | bytes 64421888 | tf_op jit(solution)/shard_map/dot_general | solution.py:11
  484.0 15.1 %convolution_convert_fusion.4 = bf16[896,2304]{1,0:T(8,128)(2,1)} fusion(bf16[2048,2304]{1,0:T(8,128)(2,1)} %get-tuple-element.16, bf16[1,2048,896]{1,2,0:T(8,128)(2,1)} %copy.23, f32[2048]{0:T(1024)S(1)} %copy-done.18), kind=kOutput, calls=%fused_computation.42 | convolution fusion | flops 8463286272 | bytes 17244160 | tf_op jit(solution)/shard_map/dot_general | solution.py:11
  499.0 10.3 %convolution_convert_fusion.5 = bf16[896,2304]{1,0:T(8,128)(2,1)} fusion(bf16[2048,2304]{1,0:T(8,128)(2,1)S(1)} %copy-done.21, bf16[1,2048,896]{1,2,0:T(8,128)(2,1)S(1)} %copy-done, f32[2048]{0:T(1024)S(1)} %copy-done.18), kind=kOutput, calls=%fused_computation.43 | convolution fusion | flops 8463286272 | bytes 17244160 | tf_op jit(solution)/shard_map/dot_general | solution.py:11
  509.3 8.6 %reshape.100 = bf16[32,504,128]{2,1,0:T(8,128)(2,1)} reshape(bf16[896,2304]{1,0:T(8,128)(2,1)} %convolution_convert_fusion.5) | data formatting | bytes 8257536 | tf_op jit(solution)/shard_map/reshape | solution.py:54
  517.9 8.6 %reshape.101 = bf16[32,504,128]{2,1,0:T(8,128)(2,1)} reshape(bf16[896,2304]{1,0:T(8,128)(2,1)} %convolution_convert_fusion.4) | data formatting | bytes 8257536 | tf_op jit(solution)/shard_map/reshape | solution.py:54
  526.5 8.2 %reshape.102 = bf16[32,504,128]{2,1,0:T(8,128)(2,1)} reshape(bf16[2304,896]{1,0:T(8,128)(2,1)} %convolution_convert_fusion.6) | data formatting | bytes 8257536 | tf_op jit(solution)/shard_map/reshape | solution.py:54
  534.8 8.4 %reshape.105 = bf16[32,504,128]{2,1,0:T(8,128)(2,1)} reshape(bf16[2304,896]{1,0:T(8,128)(2,1)} %fusion.19) | data formatting | bytes 8257536 | tf_op jit(solution)/shard_map/reshape | solution.py:54
  543.2 5.1 constant_dynamic-update-slice_fusion.5
  548.3 2.6 constant_dynamic-update-slice_fusion.4
  551.0 2.7 constant_dynamic-update-slice_fusion.3
  553.7 2.7 constant_dynamic-update-slice_fusion.2
  556.4 2.8 constant_dynamic-update-slice_fusion.1
  559.2 2.7 constant_dynamic-update-slice_fusion
  561.9 0.0 reduce-scatter.2.cloned.1.call-update
  561.9 12.7 %fusion.43 = bf16[2048,896]{0,1:T(8,128)(2,1)S(1)} fusion(bf16[2048,2304]{1,0:T(8,128)(2,1)} %get-tuple-element.17, bf16[896,2304]{1,0:T(8,128)(2,1)} %reshape_squeeze.27), kind=kOutput, calls=%fused_computation.74 | convolution fusion | flops 8455716864 | bytes 17235968 | tf_op jit(solution)/shard_map/dot_general | solution.py:11
  574.6 0.0 copy-start.16
  574.7 12.0 %fusion.14 = (f32[2048]{0:T(1024)S(1)}, bf16[2048,896]{0,1:T(8,128)(2,1)S(1)}) fusion(bf16[1,2048,896]{1,2,0:T(8,128)(2,1)S(1)} %copy-done.1, bf16[2048,896]{0,1:T(8,128)(2,1)S(1)} %fusion.43, bf16[2048,2304]{1,0:T(8,128)(2,1)} %get-tuple-element.16, bf16[896,2304]{1,0:T(8,128)(2,1)S(1)} %copy-done.9), kind=kOutput, calls=%fused_computation.34 | convolution fusion | flops 8466724864 | bytes 24584192 | tf_op jit(solution)/shard_map/dot_general | solution.py:11
  586.8 4.6 fusion.22
  591.4 6.0 copy.28
  597.4 203.7 %reduce-scatter.2.cloned.1.call-done = bf16[3024,128]{1,0:T(8,128)(2,1)} async-done(((bf16[96768,128]{1,0:T(8,128)(2,1)}), bf16[3024,128]{1,0:T(8,128)(2,1)}) %reduce-scatter.2.cloned.1.call-update) | async-done | bytes 774160 | tf_op jit(solution)/shard_map/reduce_scatter | solution.py:58
  801.1 1.2 fusion.41
  802.3 1.0 reshape_squeeze.35
  803.3 0.3 reshape_squeeze.34
  803.6 1.0 copy.30
  804.6 0.3 reshape_squeeze.33
  804.9 1.0 copy.29
  (52 shorter events, 0.1 us)
Async XLA Ops:
  7.2 159.4 %all-gather.2.cloned.1.call-start = ((), (), s32[]{:S(2)}) async-start(), calls=%async_computation.1 | async-start | bytes 25546752 | tf_op jit(solution)/shard_map/all_gather | solution.py:34
  12.2 788.9 %reduce-scatter.2.cloned.1.call-start = ((), (), s32[]{:S(2)}) async-start(), calls=%async_computation.2 | async-start | bytes 25546752 | tf_op jit(solution)/shard_map/reduce_scatter | solution.py:58
  27.2 0.6 copy-start.15
  27.8 225.3 %copy-start.17 = (f32[2048]{0:T(1024)}, f32[2048]{0:T(1024)S(1)}, u32[]{:S(2)}) copy-start(f32[2048]{0:T(1024)S(1)} %add_rsqrt_fusion.1) | copy-start | bytes 24580
  274.4 14.0 %copy-start.12 = (bf16[896,2304]{1,0:T(8,128)(2,1)S(1)}, bf16[896,2304]{1,0:T(8,128)(2,1)}, u32[]{:S(2)}) copy-start(bf16[896,2304]{1,0:T(8,128)(2,1)} %reshape_squeeze.32) | copy-start | bytes 12386308
  288.4 13.5 %copy-start.13 = (bf16[2048,896]{0,1:T(8,128)(2,1)}, bf16[2048,896]{0,1:T(8,128)(2,1)S(1)}, u32[]{:S(2)}) copy-start(bf16[2048,896]{0,1:T(8,128)(2,1)S(1)} %get-tuple-element.32) | copy-start | bytes 11010052
  288.4 13.5 %copy-start.19 = (f32[2048]{0:T(1024)}, f32[2048]{0:T(1024)S(1)}, u32[]{:S(2)}) copy-start(f32[2048]{0:T(1024)S(1)} %get-tuple-element.31) | copy-start | bytes 24580
  288.4 13.5 %copy-start.10 = (bf16[896,2304]{1,0:T(8,128)(2,1)S(1)}, bf16[896,2304]{1,0:T(8,128)(2,1)}, u32[]{:S(2)}) copy-start(bf16[896,2304]{1,0:T(8,128)(2,1)} %reshape_squeeze.31) | copy-start | bytes 12386308
  366.5 12.7 %copy-start.14 = (bf16[2048,896]{0,1:T(8,128)(2,1)S(1)}, bf16[2048,896]{0,1:T(8,128)(2,1)}, u32[]{:S(2)}) copy-start(bf16[2048,896]{0,1:T(8,128)(2,1)} %copy-done.13) | copy-start | bytes 11010052
  366.5 26.4 %slice-start = ((s8[9437184]{0:T(1024)(128)(4,1)}), s8[4194304]{0:T(1024)(128)(4,1)S(1)}, s32[]{:S(2)}) async-start(s8[9437184]{0:T(1024)(128)(4,1)} %bitcast.83), calls=%async_computation.3 | async-start | bytes 8388608
  366.5 26.4 %slice-start.1 = ((s8[9437184]{0:T(1024)(128)(4,1)}), s8[4194304]{0:T(1024)(128)(4,1)S(1)}, s32[]{:S(2)}) async-start(s8[9437184]{0:T(1024)(128)(4,1)} %bitcast.83), calls=%async_computation.4 | async-start | bytes 8388608
  379.3 13.7 %slice-start.2 = ((s8[9437184]{0:T(1024)(128)(4,1)}), s8[1048576]{0:T(1024)(128)(4,1)S(1)}, s32[]{:S(2)}) async-start(s8[9437184]{0:T(1024)(128)(4,1)} %bitcast.83), calls=%async_computation.5 | async-start | bytes 2097152
  392.9 10.5 %copy-start.11 = (bf16[896,2304]{1,0:T(8,128)(2,1)S(1)}, bf16[896,2304]{1,0:T(8,128)(2,1)}, u32[]{:S(2)}) copy-start(bf16[896,2304]{1,0:T(8,128)(2,1)} %reshape_squeeze.31) | copy-start | bytes 12386308
  413.9 17.2 %copy-start.20 = (f32[2048]{0:T(1024)S(1)}, f32[2048]{0:T(1024)}, u32[]{:S(2)}) copy-start(f32[2048]{0:T(1024)} %copy-done.19) | copy-start | bytes 24580
  438.0 15.3 %copy-start.7 = (bf16[2048,896]{0,1:T(8,128)(2,1)}, bf16[2048,896]{0,1:T(8,128)(2,1)S(1)}, u32[]{:S(2)}) copy-start(bf16[2048,896]{0,1:T(8,128)(2,1)S(1)} %fusion.23) | copy-start | bytes 11010052
  453.3 30.7 %copy-start.18 = (f32[2048]{0:T(1024)S(1)}, f32[2048]{0:T(1024)}, u32[]{:S(2)}) copy-start(f32[2048]{0:T(1024)} %copy-done.17) | copy-start | bytes 24580
  484.0 15.1 %copy-start = (bf16[1,2048,896]{1,2,0:T(8,128)(2,1)S(1)}, bf16[1,2048,896]{1,2,0:T(8,128)(2,1)}, u32[]{:S(2)}) copy-start(bf16[1,2048,896]{1,2,0:T(8,128)(2,1)} %copy.23) | copy-start | bytes 11010052
  484.0 15.1 %copy-start.21 = (bf16[2048,2304]{1,0:T(8,128)(2,1)S(1)}, bf16[2048,2304]{1,0:T(8,128)(2,1)}, u32[]{:S(2)}) copy-start(bf16[2048,2304]{1,0:T(8,128)(2,1)} %get-tuple-element.17) | copy-start | bytes 28311556
  543.2 5.2 copy-start.6
  543.2 7.8 copy-start.5
  548.3 5.4 copy-start.3
  551.0 5.4 copy-start.2
  553.7 5.5 copy-start.4
  561.9 12.7 %copy-start.1 = (bf16[1,2048,896]{1,2,0:T(8,128)(2,1)S(1)}, bf16[1,2048,896]{1,2,0:T(8,128)(2,1)}, u32[]{:S(2)}) copy-start(bf16[1,2048,896]{1,2,0:T(8,128)(2,1)} %copy.23) | copy-start | bytes 11010052
  561.9 12.7 %copy-start.9 = (bf16[896,2304]{1,0:T(8,128)(2,1)S(1)}, bf16[896,2304]{1,0:T(8,128)(2,1)}, u32[]{:S(2)}) copy-start(bf16[896,2304]{1,0:T(8,128)(2,1)} %reshape_squeeze.28) | copy-start | bytes 12386308
  574.6 12.1 %copy-start.16 = (f32[2048]{0:T(1024)S(1)}, f32[2048]{0:T(1024)}, u32[]{:S(2)}) copy-start(f32[2048]{0:T(1024)} %copy-done.15) | copy-start | bytes 24580
  574.7 12.1 %copy-start.8 = (bf16[2048,896]{0,1:T(8,128)(2,1)S(1)}, bf16[2048,896]{0,1:T(8,128)(2,1)}, u32[]{:S(2)}) copy-start(bf16[2048,896]{0,1:T(8,128)(2,1)} %copy-done.7) | copy-start | bytes 11010052
Sparse Core Ops, SparseCore 0:
  12.3 154.2 all-gather.1
  562.0 238.9 reduce-scatter.1

commit v2 on v1

v2 whole, which is shorter than its diff:
```python
import functools

import jax
import jax.numpy as jnp
from jax import lax
from jax.experimental import pallas as pl
from jax.experimental.pallas import tpu as pltpu
from jax.sharding import PartitionSpec as P

EPS = 1e-6
F32, BF16 = jnp.float32, jnp.bfloat16
MESH = pl.DeviceIdType.MESH
ANY = pl.BlockSpec(memory_space=pl.ANY)
VMEM_LIMIT = 66_000_000


class Place:
    def __init__(self):
        me = lax.axis_index("dp")
        core, z = lax.rem(me, 2), lax.rem(me // 2, 4)
        column = me - 2 * z - core
        y, x = lax.rem(me // 8, 2), me // 16
        self.me, self.core, self.z = me, core, z
        self.partner = me + 1 - 2 * core
        self.by_x, self.by_y = me + 16 - 32 * x, me + 8 - 16 * y
        over_x, over_y = column + 16 - 32 * x, column + 8 - 16 * y
        self.columns = column, over_x, over_y, over_x + 8 - 16 * y
        self.in_z = [column + core + 2 * lax.rem(z + k, 4) for k in range(4)]

    def piece(self, kind, k, core=None):
        core = self.core if core is None else core
        return self.columns[kind] + 2 * lax.rem(self.z + 4 - k, 4) + core

    def greet(self):
        barrier = pltpu.get_barrier_semaphore()
        for other in (self.partner, self.by_x, self.by_y, *self.in_z[1:]):
            pl.semaphore_signal(barrier, inc=1, device_id={"dp": other}, device_id_type=MESH)
        pl.semaphore_wait(barrier, 6)


def remote(src, dst, send, recv, device):
    return pltpu.make_async_remote_copy(
        src_ref=src, dst_ref=dst, send_sem=send, recv_sem=recv, device_id={"dp": device}, device_id_type=MESH
    )


OWN, X, Y, DIAG = range(4)


class Gather:
    def __init__(self, place, src, out, send, recv, pair, local):
        self.place, self.src, self.out = place, src, out
        self.send, self.recv, self.pair, self.local = send, recv, pair, local

    def push(self, src, at, kind, k, device):
        remote(src, self.out.at[at], self.send, self.recv.at[4 * kind + k], device).start()

    def pass_on(self, src, at):
        remote(src, self.out.at[at], self.send, self.pair, self.place.partner).start()

    def start(self):
        place = self.place
        pltpu.make_async_copy(self.src, self.out.at[place.me], self.local).start()
        for k in (1, 2, 3):
            self.push(self.src, place.me, OWN, k, place.in_z[k])
        self.push(self.src, place.me, X, 0, place.by_x)
        self.push(self.src, place.me, Y, 0, place.by_y)
        self.pass_on(self.src, place.me)

    def arrived(self, kind, k):
        at = self.place.piece(kind, k)
        here = self.out.at[at]
        pltpu.make_async_copy(here, here, self.recv.at[4 * kind + k]).wait()
        return here, at

    def along_z(self, k):
        here, at = self.arrived(OWN, k)
        self.push(here, at, X, k, self.place.by_x)
        self.push(here, at, Y, k, self.place.by_y)
        self.pass_on(here, at)

    def across(self, k):
        here, at = self.arrived(X, k)
        if k < 2:
            self.push(here, at, DIAG, k, self.place.by_y)
        self.pass_on(here, at)
        here, at = self.arrived(Y, k)
        if k >= 2:
            self.push(here, at, DIAG, k, self.place.by_x)
        self.pass_on(here, at)

    def diagonal(self, k):
        self.pass_on(*self.arrived(DIAG, k))

    def finish(self):
        pltpu.make_async_copy(self.src, self.src, self.local).wait()
        for n, sem in ((16, self.pair), (31, self.send)):
            some = self.out.at[pl.ds(0, n)]
            pltpu.make_async_copy(some, some, sem).wait()

    def events(self):
        steps = [functools.partial(self.across, 0)]
        for k in (1, 2, 3):
            steps += [functools.partial(self.along_z, k), functools.partial(self.across, k)]
        return steps + [functools.partial(self.diagonal, k) for k in range(4)]


GATHER_SEMS = (pltpu.SemaphoreType.DMA, pltpu.SemaphoreType.DMA((16,)), pltpu.SemaphoreType.DMA, pltpu.SemaphoreType.DMA)


def woven(lists, lag):
    order = [(i + lag * n, n, step) for n, steps in enumerate(lists) for i, step in enumerate(steps)]
    return [step for _, _, step in sorted(order, key=lambda t: t[:2])]


class Scatter:
    def __init__(self, place, terms, out, mine, got, send, load, pair, cross, local):
        self.place, self.terms, self.out, self.mine, self.got = place, terms, out, mine, got
        self.send, self.load, self.pair, self.cross, self.local = send, load, pair, cross, local

    def start(self):
        place = self.place
        for kind in (DIAG, X, Y, OWN):
            for k in range(4):
                slot = 4 * kind + k
                src = self.terms.at[place.piece(kind, k, 1 - place.core)]
                remote(src, self.got.at[slot], self.send, self.pair.at[kind], place.partner).start()
                pltpu.make_async_copy(self.terms.at[place.piece(kind, k)], self.mine.at[slot], self.load.at[kind]).start()

    def ready(self, kind):
        four = self.mine.at[pl.ds(0, 4)]
        pltpu.make_async_copy(four, four, self.load.at[kind]).wait()
        pltpu.make_async_copy(four, four, self.pair.at[kind]).wait()

    def total(self, kind, k, others):
        slot = 4 * kind + k
        for n in others:
            here = self.got.at[16 + n]
            pltpu.make_async_copy(here, here, self.cross.at[n]).wait()
        total = self.mine[slot].astype(F32) + self.got[slot].astype(F32)
        for n in others:
            total += self.got[16 + n].astype(F32)
        return total.astype(BF16)

    def push(self, kind, k, others, to, device):
        slot = 4 * kind + k
        self.mine[slot] = self.total(kind, k, others)
        remote(self.mine.at[slot], self.got.at[16 + to], self.send, self.cross.at[to], device).start()

    def diagonal(self):
        self.ready(DIAG)
        for k in range(4):
            self.push(DIAG, k, (), k, self.place.by_x if k < 2 else self.place.by_y)

    def straight(self):
        self.ready(X)
        self.ready(Y)
        for k in (0, 1):
            self.push(X, k, (), 4 + k, self.place.by_x)
        for k in (2, 3):
            self.push(Y, k, (), 8 + k, self.place.by_y)

    def across(self):
        for k in (0, 1):
            self.push(Y, k, (k,), 8 + k, self.place.by_y)
        for k in (2, 3):
            self.push(X, k, (k,), 4 + k, self.place.by_x)

    def along_z(self):
        self.ready(OWN)
        for k in (1, 2, 3):
            self.push(OWN, k, (4 + k, 8 + k), 12 + k, self.place.in_z[4 - k])

    def last(self):
        self.mine[0] = self.total(OWN, 0, (4, 8, 13, 14, 15))
        pltpu.make_async_copy(self.mine.at[0], self.out, self.local).start()

    def events(self):
        return [self.diagonal, self.straight, self.across, self.along_z, self.last]

    def finish(self):
        pltpu.make_async_copy(self.mine.at[0], self.out, self.local).wait()
        some = self.terms.at[pl.ds(0, 31)]
        pltpu.make_async_copy(some, some, self.send).wait()


def scatter_scratch(terms):
    block = terms.shape[1:]
    dma = pltpu.SemaphoreType.DMA
    return [pltpu.VMEM((16, *block), BF16), pltpu.VMEM((32, *block), BF16), dma, dma((4,)), dma((4,)), dma((16,)), dma]


class Comm:
    def __init__(self, kind, arrays):
        self.kind, self.arrays, self.n = kind, list(arrays), len(arrays)
        if kind == "gather":
            self.shapes = [jax.ShapeDtypeStruct((32, *b.shape), BF16) for b in arrays]
            self.scratch = [s for _ in arrays for s in GATHER_SEMS]
        else:
            self.shapes = [jax.ShapeDtypeStruct(t.shape[1:], BF16) for t in arrays]
            self.scratch = [s for t in arrays for s in scatter_scratch(t)]
        self.specs = [ANY] * self.n

    def make(self, srcs, outs, scratch):
        place = Place()
        one = Gather if self.kind == "gather" else Scatter
        per = len(scratch) // max(self.n, 1)
        return place, [one(place, srcs[i], outs[i], *scratch[per * i : per * (i + 1)]) for i in range(self.n)]

    def drive(self, srcs, outs, scratch, step, steps):
        if not self.n:
            return
        place, ones = self.make(srcs, outs, scratch)
        events = woven([one.events() for one in ones], 3 if self.kind == "gather" else 1)

        @pl.when(step == 0)
        def _():
            place.greet()
            for one in ones:
                one.start()

        for i in range(steps):
            lo, hi = len(events) * i // steps, len(events) * (i + 1) // steps

            @pl.when(step == i)
            def _(lo=lo, hi=hi):
                for event in events[lo:hi]:
                    event()

        @pl.when(step == steps - 1)
        def _():
            for one in ones:
                one.finish()


NONE = Comm("gather", ())


def call(body, name, grid, ins, in_specs, outs, out_specs, scratch, comm, number, flops):
    n_in, n_out, n_scratch = len(ins), len(outs), len(scratch)

    def kernel(*refs):
        step = pl.program_id(0)
        cut = [n_in, comm.n, n_out, comm.n, n_scratch, len(comm.scratch)]
        groups, at = [], 0
        for c in cut:
            groups.append(refs[at : at + c])
            at += c
        srcs, sent = groups[1], groups[3]
        if body is not None:
            body(step, groups[0], groups[2], groups[4])
        comm.drive(srcs, sent, groups[5], step, grid)

    params = dict(vmem_limit_bytes=VMEM_LIMIT, dimension_semantics=("arbitrary",))
    if comm.n:
        params |= dict(collective_id=number, has_side_effects=True)
    results = pl.pallas_call(
        kernel,
        grid=(grid,),
        out_shape=[*outs, *comm.shapes],
        in_specs=[*in_specs, *comm.specs],
        out_specs=[*out_specs, *comm.specs],
        scratch_shapes=[*scratch, *comm.scratch],
        compiler_params=pltpu.CompilerParams(**params),
        cost_estimate=pl.CostEstimate(flops=flops, bytes_accessed=50_000_000, transcendentals=0),
        name=name,
    )(*ins, *comm.arrays)
    return list(results[:n_out]), list(results[n_out:])


def whole(shape):
    return pl.BlockSpec(shape, lambda i: (0,) * len(shape), pipeline_mode=pl.Buffered(1))


def over(rows, columns):
    return pl.BlockSpec((rows, columns), lambda i: (i, 0))


def across(rows, columns):
    return pl.BlockSpec((rows, columns), lambda i: (0, i))


def like(shape, dtype=BF16):
    return jax.ShapeDtypeStruct(shape, dtype)


def dot(a, b, ca, cb):
    return lax.dot_general(a, b, (((ca,), (cb,)), ((), ())), preferred_element_type=F32)


TILE = 256


def close_up(blocks, out):
    n, rows, _ = blocks.shape

    def pair(i, _):
        two = jnp.concatenate([blocks[2 * i].astype(F32), blocks[2 * i + 1].astype(F32)], 0)
        out[pl.ds(pl.multiple_of(2 * rows * i, 8), 2 * rows), :] = two.astype(BF16)
        return 0

    lax.fori_loop(0, n // 2, pair, 0)


def forward(h, wg, wu, wd, comm, number):
    tokens, d = h.shape
    n, rows, ff = wg.shape
    piece = ff // 3

    def body(step, ins, outs, scratch):
        h_ref, wg_ref, wu_ref, wd_ref = ins
        h_out, gate_ref, up_ref, pt_ref, at_ref, wg_out, wu_out = outs
        (p_ref,) = scratch

        @pl.when(step == 0)
        def _():
            close_up(wg_ref, wg_out)
            close_up(wu_ref, wu_out)

        wide = h_ref[...].astype(F32)
        a = (wide * lax.rsqrt(jnp.mean(wide**2, -1, keepdims=True) + EPS)).astype(BF16)
        at_ref[...] = a.T
        for c in range(3):
            part = pl.ds(piece * c, piece)
            gate = dot(a, wg_out[:, part], 1, 0)
            up = dot(a, wu_out[:, part], 1, 0)
            gate_ref[:, part] = gate
            up_ref[:, part] = up
            p = (gate * jax.nn.sigmoid(gate) * up).astype(BF16)
            p_ref[:, part] = p
            pt_ref[part, :] = p.T
        h_out[...] = h_ref[...] + dot(p_ref[...], wd_ref[...], 1, 0).astype(BF16)

    return call(
        body, f"forward_{number}", tokens // TILE,
        (h, wg, wu, wd),
        (over(TILE, d), whole(wg.shape), whole(wu.shape), whole(wd.shape)),
        (like(h.shape), like((tokens, ff), F32), like((tokens, ff), F32), like((ff, tokens)), like((d, tokens)),
         like((d, ff)), like((d, ff))),
        (over(TILE, d), over(TILE, ff), over(TILE, ff), across(ff, TILE), across(d, TILE), whole((d, ff)), whole((d, ff))),
        (pltpu.VMEM((TILE, ff), BF16),),
        comm, number, 6 * tokens * d * ff,
    )


def backward(by_h, h, gate, up, wg, wu, wd, comm, number):
    tokens, d = h.shape
    ff = gate.shape[1]
    piece = ff // 3

    def body(step, ins, outs, scratch):
        by_ref, h_ref, gate_ref, up_ref, wg_ref, wu_ref, wd_ref = ins
        by_gate_ref, by_up_ref, by_h_out = outs
        by_h = by_ref[...]
        for c in range(3):
            part = pl.ds(piece * c, piece)
            by_p = dot(by_h, wd_ref[part, :], 1, 1).astype(BF16).astype(F32)
            gate, up = gate_ref[:, part], up_ref[:, part]
            s = jax.nn.sigmoid(gate)
            by_up_ref[:, part] = (by_p * (gate * s)).astype(BF16)
            by_gate_ref[:, part] = (by_p * up * (s * (1 + gate * (1 - s)))).astype(BF16)
        by_a = dot(by_gate_ref[...], wg_ref[...], 1, 1).astype(BF16) + dot(by_up_ref[...], wu_ref[...], 1, 1).astype(BF16)
        wide, by_a = h_ref[...].astype(F32), by_a.astype(F32)
        scale = lax.rsqrt(jnp.mean(wide**2, -1, keepdims=True) + EPS)
        inner = jnp.mean(by_a * wide, -1, keepdims=True)
        by_h_out[...] = by_h + (scale * (by_a - wide * (scale * scale * inner))).astype(BF16)

    tile_d, tile_ff = over(TILE, d), over(TILE, ff)
    return call(
        body, f"backward_{number}", tokens // TILE,
        (by_h, h, gate, up, wg, wu, wd),
        (tile_d, tile_d, tile_ff, tile_ff, whole(wg.shape), whole(wu.shape), whole(wd.shape)),
        (like((tokens, ff)), like((tokens, ff)), like(h.shape)),
        (tile_ff, tile_ff, tile_d),
        (), comm, number, 6 * tokens * d * ff,
    )


def weight_terms(at, pt, by_gate, by_up, by_h, rows, comm, number):
    d, tokens = at.shape
    ff = pt.shape[0]
    n = d // rows

    def body(step, ins, outs, scratch):
        at_ref, pt_ref, by_gate_ref, by_up_ref, by_h_ref = ins
        wg_ref, wu_ref, wd_ref = outs
        for by_ref, w_ref in ((by_gate_ref, wg_ref), (by_up_ref, wu_ref)):
            term = dot(at_ref[...], by_ref[...], 1, 0)
            for j in range(n):
                w_ref[j] = term[rows * j : rows * j + rows].astype(BF16)
        wd_ref[...] = dot(pt_ref[...], by_h_ref[...], 1, 0).astype(BF16)

    blocks = pl.BlockSpec((n, rows, TILE), lambda i: (0, 0, i))
    return call(
        body, f"weight_terms_{number}", ff // TILE,
        (at, pt, by_gate, by_up, by_h),
        (whole(at.shape), over(TILE, tokens), across(tokens, TILE), across(tokens, TILE), whole(by_h.shape)),
        (like((n, rows, ff)), like((n, rows, ff)), like((ff, d))),
        (blocks, blocks, over(TILE, d)),
        (), comm, number, 6 * tokens * d * ff,
    )


def solution(mesh):
    def step(x, dy, w_gate, w_up, w_down):
        layers, rows, ff = w_gate.shape
        d = w_down.shape[2]
        own = [Comm("gather", (w_gate[n], w_up[n], w_down[n])) for n in range(layers)]
        _, held = call(None, "gather", 1, (), (), (), (), (), own[0], 0, 0)
        h, by_h = x[0], dy[0]
        kept = []
        for n in range(layers):
            wd = held[2].reshape(ff, d)
            (after, gate, up, pt, at, wg, wu), coming = forward(h, held[0], held[1], wd, own[n + 1] if n + 1 < layers else NONE, 1 + n)
            kept.append((h, gate, up, pt, at, wg, wu, wd))
            h, held = after, coming
        by_weights, terms = [], None
        for n in reversed(range(layers)):
            h, gate, up, pt, at, wg, wu, wd = kept[n]
            comm = NONE if terms is None else Comm("scatter", terms)
            (by_gate, by_up, before), summed = backward(by_h, h, gate, up, wg, wu, wd, comm, 8 + n)
            if terms is not None:
                by_weights.insert(0, summed)
            terms, _ = weight_terms(at, pt, by_gate, by_up, by_h, rows, NONE, 16 + n)
            terms[2] = terms[2].reshape(-1, *w_down.shape[1:])
            by_h = before
        _, summed = call(None, "scatter", 1, (), (), (), (), (), Comm("scatter", terms), 24, 0)
        by_weights.insert(0, summed)
        return (by_h[None], *(jnp.stack(t) for t in zip(*by_weights)))

    tokens, weights = P(("rep", "dp"), None, None), P(None, "dp", None)
    sums = P("rep", "dp", None)
    return jax.shard_map(
        step,
        mesh=mesh,
        in_specs=(tokens, tokens, weights, weights, weights),
        out_specs=(tokens, sums, sums, sums),
        check_vma=False,
    )
```

time: 823 us -> 520 us (0.63); the launches traced: 813 us -> 520 us
  Pallas kernels: 0 us -> 503 us
  waiting for transfers between devices: 343 us -> 0 us
  matrix products: 274 us -> 0 us
  local copies, waits for them, and re-layouts: 168 us -> 12.3 us
  between operations: 14.6 us -> 0.71 us
  other arithmetic: 14.4 us -> 3.52 us
    pallas_call x0 -> x8, Pallas kernels: none -> 503 us  [call(): pl.pallas_call(kernel, grid=(grid,), out_shape=[*outs, *comm.shapes], in_...]
    dot_general x17 -> x0, matrix products: 274 us -> none  [dot(): lax.dot_general(a, b, (((ca,), (cb,)), ((), ())), preferred_element_type=...]
    reduce_scatter x1 -> x0, waiting for transfers between devices: 204 us -> none  [step(): lax.psum_scatter(sent, 'dp', scatter_dimension=0, tiled=True)]
    all_gather x1 -> x0, waiting for transfers between devices: 139 us -> none  [step(): lax.all_gather(jnp.concatenate(parts, 1).reshape(layers * 3 * size, 128),...]
    reshape x9 -> x0, local copies, waits for them, and re-layouts: 52.9 us -> none  [the longest x6 51 us: step(): t.astype(BF16).reshape(devices, size, 128)]
    another operation x9 -> x0, local copies, waits for them, and re-layouts: 52.1 us -> none  [the longest x4 33.9 us: step(): wg, wu = (held[:, n, k].reshape(devices * rows, ff) for k in (0, 1))]
    unnamed x62 -> x9, local copies, waits for them, and re-layouts: 38.8 us -> 6.1 us
    slice x2, local copies, waits for them, and re-layouts: 20.2 us -> 3.03 us  [the longest x1 1.52 us: step(): w_gate[n]]
  transfers between devices with their start and end apart: 2 -> 0, of which waited for: 2 -> 0; matrix products, arithmetic and copies ran while one was open for 6% -> 0% of each run, Pallas kernels for 0% -> 0%
where the time goes in v2:
time: 520 us
  Pallas kernels  503 us (97%)
  local copies, waits for them, and re-layouts  12.3 us (2%)
    pallas_call x8, Pallas kernels, call(): pl.pallas_call(kernel, grid=(grid,), out_shape=[*outs, *comm.shapes], in_...  503 us

profile of v2, /device:TPU:0, one launch (start us, length us, event | category | flops | bytes accessed | tf_op | source)
XLA Modules:
  0.0 519.7 jit_solution(12360963055685437017)
XLA Ops:
  0.6 1.7 slice_bitcast_fusion
  2.3 1.5 fusion.1
  3.8 0.8 copy_bitcast_fusion.1
  4.6 1.5 fusion
  6.1 0.8 copy_bitcast_fusion
  6.9 74.1 %gather.1 = (bf16[32,28,2304]{2,1,0:T(8,128)(2,1)}, bf16[32,28,2304]{2,1,0:T(8,128)(2,1)}, bf16[32,72,896]{2,1,0:T(8,128)(2,1)}) custom-call(bf16[28,2304]{1,0:T(8,128)(2,1)} %get-tuple-element.89.refs_0_, bf16[28,2304]{1,0:T(8,128)(2,1)} %get-tuple-element.91.refs_1_, bf16[72,896]{1,0:T(8,128)(2,1)} %get-tuple-element.83.refs_2_), custom_call_target="tpu_custom_call" | custom-call | bytes 50000000 | tf_op jit(solution)/shard_map/gather/pallas_call | solution.py:257
  81.0 99.6 %forward_1.1 = (bf16[2048,896]{1,0:T(8,128)(2,1)}, f32[2048,2304]{1,0:T(8,128)}, f32[2048,2304]{1,0:T(8,128)}, bf16[2304,2048]{1,0:T(8,128)(2,1)}, bf16[896,2048...) custom-call(bf16[2048,896]{1,0:T(8,128)(2,1)} %bitcast.37, ...), custom_call_target="tpu_custom_call" | custom-call | flops 25367150592 | bytes 50000000 | tf_op jit(solution)/shard_map/forward_1/pallas_call | solution.py:257
  180.6 43.0 %forward_2.1 = (bf16[2048,896]{1,0:T(8,128)(2,1)}, f32[2048,2304]{1,0:T(8,128)}, f32[2048,2304]{1,0:T(8,128)}, bf16[2304,2048]{1,0:T(8,128)(2,1)}, bf16[896,2048...) custom-call(bf16[2048,896]{1,0:T(8,128)(2,1)} %get-tuple-element.44.refs_0_.refs_1_, ...), custom_call_target="tpu_custom_call" | custom-call | flops 25367150592 | bytes 50000000 | tf_op jit(solution)/shard_map/forward_2/pallas_call | solution.py:257
  223.5 42.7 %backward_9.1 = (bf16[2048,2304]{1,0:T(8,128)(2,1)}, bf16[2048,2304]{1,0:T(8,128)(2,1)}, bf16[2048,896]{1,0:T(8,128)(2,1)}) custom-call(bf16[2048,896]{1,0:T(8,128)(2,1)} %bitcast.35, bf16[2048,896]{1,0:T(8,128)(2,1)} %get-tuple-element.44.refs_0_.refs_1_, f32[2048,2304]{1,0:T(8,128)} %get-tuple-element.48.refs_2_, f32[2048,2304]{1,0:T(8,128)} %get-tuple-element.49.refs_3_, ...), custom_call_target="tpu_custom_call" | custom-call | flops 25367150592 | bytes 50000000 | tf_op jit(solution)/shard_map/backward_9/pallas_call | solution.py:257
  266.2 34.0 %weight_terms_17.1 = (bf16[32,28,2304]{2,1,0:T(8,128)(2,1)}, bf16[32,28,2304]{2,1,0:T(8,128)(2,1)}, bf16[2304,896]{1,0:T(8,128)(2,1)}) custom-call(bf16[896,2048]{1,0:T(8,128)(2,1)} %get-tuple-element.57.refs_0_, bf16[2304,2048]{1,0:T(8,128)(2,1)} %get-tuple-element.58.refs_1_, bf16[2048,2304]{1,0:T(8,128)(2,1)} %get-tuple-element.59.refs_2_, ...), custom_call_target="tpu_custom_call" | custom-call | flops 25367150592 | bytes 50000000 | tf_op jit(solution)/shard_map/weight_terms_17/pallas_call | solution.py:257
  300.2 98.2 %backward_8.1 = (bf16[2048,2304]{1,0:T(8,128)(2,1)}, bf16[2048,2304]{1,0:T(8,128)(2,1)}, bf16[2048,896]{1,0:T(8,128)(2,1)}, bf16[28,2304]{1,0:T(8,128)(2,1)}, bf...) custom-call(bf16[2048,896]{1,0:T(8,128)(2,1)} %get-tuple-element.52.refs_0_.refs_4_, bf16[2048,896]{1,0:T(8,128)(2,1)} %bitcast.38, ...), custom_call_target="tpu_custom_call" | custom-call | flops 25367150592 | bytes 50000000 | tf_op jit(solution)/shard_map/backward_8/pallas_call | solution.py:257
  398.4 33.8 %weight_terms_16.1 = (bf16[32,28,2304]{2,1,0:T(8,128)(2,1)}, bf16[32,28,2304]{2,1,0:T(8,128)(2,1)}, bf16[2304,896]{1,0:T(8,128)(2,1)}) custom-call(bf16[896,2048]{1,0:T(8,128)(2,1)} %get-tuple-element.65.refs_0_, bf16[2304,2048]{1,0:T(8,128)(2,1)} %get-tuple-element.66.refs_1_, bf16[2048,2304]{1,0:T(8,128)(2,1)} %get-tuple-element.67.refs_2_, ...), custom_call_target="tpu_custom_call" | custom-call | flops 25367150592 | bytes 50000000 | tf_op jit(solution)/shard_map/weight_terms_16/pallas_call | solution.py:257
  432.3 0.0 copy-start.1
  432.3 0.0 copy-start
  432.3 0.0 copy-start.2
  432.3 77.8 %scatter.1 = (bf16[28,2304]{1,0:T(8,128)(2,1)}, bf16[28,2304]{1,0:T(8,128)(2,1)}, bf16[72,896]{1,0:T(8,128)(2,1)}) custom-call(bf16[32,28,2304]{2,1,0:T(8,128)(2,1)} %get-tuple-element.69.refs_0_, bf16[32,28,2304]{2,1,0:T(8,128)(2,1)} %get-tuple-element.70.refs_1_, bf16[32,72,896]{2,1,0:T(8,128)(2,1)} %bitcast.25), custom_call_target="tpu_custom_call" | custom-call | bytes 50000000 | tf_op jit(solution)/shard_map/scatter/pallas_call | solution.py:257
  510.1 0.0 copy-done.1
  510.1 0.9 pad_maximum_fusion
  511.0 1.0 copy.13
  512.0 0.0 copy-done
  512.0 0.9 pad_maximum_fusion.1
  513.0 1.0 copy.14
  513.9 0.0 copy-done.2
  513.9 1.6 pad_maximum_fusion.2
  515.5 4.2 copy.24
Async XLA Ops:
  432.3 77.8 %copy-start.1 = (bf16[28,2304]{1,0:T(8,128)(2,1)S(1)}, bf16[28,2304]{1,0:T(8,128)(2,1)}, u32[]{:S(2)}) copy-start(bf16[28,2304]{1,0:T(8,128)(2,1)} %get-tuple-element.73) | copy-start | bytes 387076
  432.3 79.7 %copy-start = (bf16[28,2304]{1,0:T(8,128)(2,1)S(1)}, bf16[28,2304]{1,0:T(8,128)(2,1)}, u32[]{:S(2)}) copy-start(bf16[28,2304]{1,0:T(8,128)(2,1)} %get-tuple-element.75) | copy-start | bytes 387076
  432.3 81.6 %copy-start.2 = (bf16[72,896]{1,0:T(8,128)(2,1)S(1)}, bf16[72,896]{1,0:T(8,128)(2,1)}, u32[]{:S(2)}) copy-start(bf16[72,896]{1,0:T(8,128)(2,1)} %get-tuple-element.77) | copy-start | bytes 387076

commit v3 on v2

v3 whole, which is shorter than its diff:
```python
import functools

import jax
import jax.numpy as jnp
from jax import lax
from jax.experimental import pallas as pl
from jax.experimental.pallas import tpu as pltpu
from jax.sharding import PartitionSpec as P

EPS = 1e-6
F32, BF16 = jnp.float32, jnp.bfloat16
MESH = pl.DeviceIdType.MESH
ANY = pl.BlockSpec(memory_space=pl.ANY)
VMEM_LIMIT = 66_000_000


class Place:
    def __init__(self):
        me = lax.axis_index("dp")
        core, z = lax.rem(me, 2), lax.rem(me // 2, 4)
        column = me - 2 * z - core
        y, x = lax.rem(me // 8, 2), me // 16
        self.me, self.core, self.z = me, core, z
        self.partner = me + 1 - 2 * core
        self.by_x, self.by_y = me + 16 - 32 * x, me + 8 - 16 * y
        over_x, over_y = column + 16 - 32 * x, column + 8 - 16 * y
        self.columns = column, over_x, over_y, over_x + 8 - 16 * y
        self.in_z = [column + core + 2 * lax.rem(z + k, 4) for k in range(4)]

    def piece(self, kind, k, core=None):
        core = self.core if core is None else core
        return self.columns[kind] + 2 * lax.rem(self.z + 4 - k, 4) + core

    def greet(self):
        barrier = pltpu.get_barrier_semaphore()
        for other in (self.partner, self.by_x, self.by_y, *self.in_z[1:]):
            pl.semaphore_signal(barrier, inc=1, device_id={"dp": other}, device_id_type=MESH)
        pl.semaphore_wait(barrier, 6)


def remote(src, dst, send, recv, device):
    return pltpu.make_async_remote_copy(
        src_ref=src, dst_ref=dst, send_sem=send, recv_sem=recv, device_id={"dp": device}, device_id_type=MESH
    )


OWN, X, Y, DIAG = range(4)


class Gather:
    def __init__(self, place, src, out, send, recv, pair, local):
        self.place, self.src, self.out = place, src, out
        self.send, self.recv, self.pair, self.local = send, recv, pair, local

    def push(self, src, at, kind, k, device):
        remote(src, self.out.at[at], self.send, self.recv.at[4 * kind + k], device).start()

    def pass_on(self, src, at):
        remote(src, self.out.at[at], self.send, self.pair, self.place.partner).start()

    def start(self):
        place = self.place
        pltpu.make_async_copy(self.src, self.out.at[place.me], self.local).start()
        for k in (1, 2, 3):
            self.push(self.src, place.me, OWN, k, place.in_z[k])
        self.push(self.src, place.me, X, 0, place.by_x)
        self.push(self.src, place.me, Y, 0, place.by_y)
        self.pass_on(self.src, place.me)

    def arrived(self, kind, k):
        at = self.place.piece(kind, k)
        here = self.out.at[at]
        pltpu.make_async_copy(here, here, self.recv.at[4 * kind + k]).wait()
        return here, at

    def along_z(self, k):
        here, at = self.arrived(OWN, k)
        self.push(here, at, X, k, self.place.by_x)
        self.push(here, at, Y, k, self.place.by_y)
        self.pass_on(here, at)

    def across(self, k):
        here, at = self.arrived(X, k)
        if k < 2:
            self.push(here, at, DIAG, k, self.place.by_y)
        self.pass_on(here, at)
        here, at = self.arrived(Y, k)
        if k >= 2:
            self.push(here, at, DIAG, k, self.place.by_x)
        self.pass_on(here, at)

    def diagonal(self, k):
        self.pass_on(*self.arrived(DIAG, k))

    def finish(self):
        pltpu.make_async_copy(self.src, self.src, self.local).wait()
        for n, sem in ((16, self.pair), (31, self.send)):
            some = self.out.at[pl.ds(0, n)]
            pltpu.make_async_copy(some, some, sem).wait()

    def events(self):
        groups = [[functools.partial(self.across, 0)]]
        for k in (1, 2, 3):
            groups += [[functools.partial(self.along_z, k)], [functools.partial(self.across, k)]]
        return groups + [[functools.partial(self.diagonal, k)] for k in range(4)]


GATHER_SEMS = (pltpu.SemaphoreType.DMA, pltpu.SemaphoreType.DMA((16,)), pltpu.SemaphoreType.DMA, pltpu.SemaphoreType.DMA)


def woven(lists, lag):
    order = [(i + lag * n, n, group) for n, groups in enumerate(lists) for i, group in enumerate(groups)]
    return [step for _, _, group in sorted(order, key=lambda t: t[:2]) for step in group]


class Scatter:
    def __init__(self, place, terms, out, columns, mine, got, send, load, pair, cross, local):
        self.place, self.mine, self.got = place, mine, got
        self.terms, self.out = terms.at[:, :, columns], out.at[:, columns]
        self.send, self.load, self.pair, self.cross, self.local = send, load, pair, cross, local

    def start(self):
        place = self.place
        for kind in (DIAG, X, Y, OWN):
            for k in range(4):
                slot = 4 * kind + k
                src = self.terms.at[place.piece(kind, k, 1 - place.core)]
                remote(src, self.got.at[slot], self.send, self.pair.at[kind], place.partner).start()
                pltpu.make_async_copy(self.terms.at[place.piece(kind, k)], self.mine.at[slot], self.load.at[kind]).start()

    def ready(self, kind):
        four = self.mine.at[pl.ds(0, 4)]
        pltpu.make_async_copy(four, four, self.load.at[kind]).wait()
        pltpu.make_async_copy(four, four, self.pair.at[kind]).wait()

    def total(self, kind, k, others):
        slot = 4 * kind + k
        for n in others:
            here = self.got.at[16 + n]
            pltpu.make_async_copy(here, here, self.cross.at[n]).wait()
        total = self.mine[slot].astype(F32) + self.got[slot].astype(F32)
        for n in others:
            total += self.got[16 + n].astype(F32)
        return total.astype(BF16)

    def push(self, kind, k, others, to, device):
        slot = 4 * kind + k
        self.mine[slot] = self.total(kind, k, others)
        remote(self.mine.at[slot], self.got.at[16 + to], self.send, self.cross.at[to], device).start()

    def diagonal(self, k):
        if k == 0:
            self.ready(DIAG)
        self.push(DIAG, k, (), k, self.place.by_x if k < 2 else self.place.by_y)

    def over_x(self, k):
        if k == 0:
            self.ready(X)
        self.push(X, k, () if k < 2 else (k,), 4 + k, self.place.by_x)

    def over_y(self, k):
        if k == 2:
            self.ready(Y)
        self.push(Y, k, (k,) if k < 2 else (), 8 + k, self.place.by_y)

    def along_z(self, k):
        if k == 1:
            self.ready(OWN)
        self.push(OWN, k, (4 + k, 8 + k), 12 + k, self.place.in_z[4 - k])

    def last(self):
        self.mine[0] = self.total(OWN, 0, (4, 8, 13, 14, 15))
        pltpu.make_async_copy(self.mine.at[0], self.out, self.local).start()

    def events(self):
        do = functools.partial
        return [
            [do(self.diagonal, k) for k in (0, 2, 1, 3)],
            [do(self.over_x, 0), do(self.over_y, 2), do(self.over_x, 1), do(self.over_y, 3)],
            [do(self.over_y, 0), do(self.over_x, 2), do(self.over_y, 1), do(self.over_x, 3)],
            [do(self.along_z, k) for k in (1, 2, 3)],
            [self.last],
        ]

    def finish(self):
        pltpu.make_async_copy(self.mine.at[0], self.out, self.local).wait()
        some = self.terms.at[pl.ds(0, 31)]
        pltpu.make_async_copy(some, some, self.send).wait()


PARTS = 2


def cuts(columns):
    at = [128 * (columns // 128 * i // PARTS) for i in range(PARTS + 1)]
    return [(lo, hi - lo) for lo, hi in zip(at, at[1:])]


def scatter_scratch(rows, columns):
    dma = pltpu.SemaphoreType.DMA
    return [
        pltpu.VMEM((16, rows, columns), BF16), pltpu.VMEM((32, rows, columns), BF16), dma, dma((4,)), dma((4,)), dma((16,)), dma
    ]


class Comm:
    def __init__(self, kind, arrays):
        self.kind, self.arrays, self.n = kind, list(arrays), len(arrays)
        if kind == "gather":
            self.shapes = [jax.ShapeDtypeStruct((32, *b.shape), BF16) for b in arrays]
            self.scratch = [s for _ in arrays for s in GATHER_SEMS]
        else:
            self.shapes = [jax.ShapeDtypeStruct(t.shape[1:], BF16) for t in arrays]
            self.scratch = [s for t in arrays for _, width in cuts(t.shape[2]) for s in scatter_scratch(t.shape[1], width)]
        self.specs = [ANY] * self.n

    def make(self, srcs, outs, scratch):
        place = Place()
        if self.kind == "gather":
            return place, [Gather(place, srcs[i], outs[i], *scratch[4 * i : 4 * i + 4]) for i in range(self.n)]
        parts = [(i, pl.ds(lo, width)) for i, t in enumerate(self.arrays) for lo, width in cuts(t.shape[2])]
        return place, [Scatter(place, srcs[i], outs[i], part, *scratch[7 * k : 7 * k + 7]) for k, (i, part) in enumerate(parts)]

    def driver(self, srcs, outs, scratch, step, steps, polls):
        if not self.n:
            return lambda: None, lambda: None
        place, ones = self.make(srcs, outs, scratch)
        events = woven([one.events() for one in ones], 3 if self.kind == "gather" else 1)
        slots, calls = steps * polls, iter(range(polls))

        @pl.when(step == 0)
        def _():
            place.greet()
            for one in ones:
                one.start()

        def poll():
            call = next(calls)
            for i in range(steps):
                slot = i * polls + call
                share = events[len(events) * slot // slots : len(events) * (slot + 1) // slots]
                if share:

                    @pl.when(step == i)
                    def _(share=share):
                        for event in share:
                            event()

        def end():
            @pl.when(step == steps - 1)
            def _():
                for one in ones:
                    one.finish()

        return poll, end


NONE = Comm("gather", ())


def call(body, name, grid, ins, in_specs, outs, out_specs, scratch, comm, number, flops, polls=1):
    n_in, n_out, n_scratch = len(ins), len(outs), len(scratch)

    def kernel(*refs):
        step = pl.program_id(0)
        cut = [n_in, comm.n, n_out, comm.n, n_scratch, len(comm.scratch)]
        groups, at = [], 0
        for c in cut:
            groups.append(refs[at : at + c])
            at += c
        poll, end = comm.driver(groups[1], groups[3], groups[5], step, grid, polls)
        body(step, groups[0], groups[2], groups[4], poll)
        end()

    params = dict(vmem_limit_bytes=VMEM_LIMIT, dimension_semantics=("arbitrary",))
    if comm.n:
        params |= dict(collective_id=number, has_side_effects=True)
    results = pl.pallas_call(
        kernel,
        grid=(grid,),
        out_shape=[*outs, *comm.shapes],
        in_specs=[*in_specs, *comm.specs],
        out_specs=[*out_specs, *comm.specs],
        scratch_shapes=[*scratch, *comm.scratch],
        compiler_params=pltpu.CompilerParams(**params),
        cost_estimate=pl.CostEstimate(flops=flops, bytes_accessed=50_000_000, transcendentals=0),
        name=name,
    )(*ins, *comm.arrays)
    return list(results[:n_out]), list(results[n_out:])


def whole(shape):
    return pl.BlockSpec(shape, lambda i: (0,) * len(shape), pipeline_mode=pl.Buffered(1))


def over(rows, columns):
    return pl.BlockSpec((rows, columns), lambda i: (i, 0))


def across(rows, columns):
    return pl.BlockSpec((rows, columns), lambda i: (0, i))


def like(shape, dtype=BF16):
    return jax.ShapeDtypeStruct(shape, dtype)


def dot(a, b, ca, cb):
    return lax.dot_general(a, b, (((ca,), (cb,)), ((), ())), preferred_element_type=F32)


TILE = 256


def close_up(blocks, out):
    n, rows, _ = blocks.shape

    def pair(i, _):
        two = jnp.concatenate([blocks[2 * i].astype(F32), blocks[2 * i + 1].astype(F32)], 0)
        out[pl.ds(pl.multiple_of(2 * rows * i, 8), 2 * rows), :] = two.astype(BF16)
        return 0

    lax.fori_loop(0, n // 2, pair, 0)


def normed(h):
    wide = h.astype(F32)
    return (wide * lax.rsqrt(jnp.mean(wide**2, -1, keepdims=True) + EPS)).astype(BF16)


def gated(by_p, gate, up):
    s = jax.nn.sigmoid(gate)
    return (by_p * up * (s * (1 + gate * (1 - s)))).astype(BF16), (by_p * (gate * s)).astype(BF16)


def forward(h, wg, wu, comm, number):
    tokens, d = h.shape
    ff = wg.shape[2]
    piece = ff // 3

    def body(step, ins, outs, scratch, poll):
        h_ref, wg_ref, wu_ref = ins
        gate_ref, up_ref, p_ref, pt_ref, at_ref, wg_out, wu_out = outs

        @pl.when(step == 0)
        def _():
            close_up(wg_ref, wg_out)
            close_up(wu_ref, wu_out)

        a = normed(h_ref[...])
        at_ref[...] = a.T
        for c in range(3):
            part = pl.ds(piece * c, piece)
            gate = dot(a, wg_out[:, part], 1, 0)
            up = dot(a, wu_out[:, part], 1, 0)
            gate_ref[:, part] = gate
            up_ref[:, part] = up
            p = (gate * jax.nn.sigmoid(gate) * up).astype(BF16)
            p_ref[:, part] = p
            pt_ref[part, :] = p.T
            if c != 1:
                poll()

    tile_d, tile_ff = over(TILE, d), over(TILE, ff)
    wide, square = like((tokens, ff), F32), like((d, ff))
    return call(
        body, f"forward_{number}", tokens // TILE,
        (h, wg, wu), (tile_d, whole(wg.shape), whole(wu.shape)),
        (wide, wide, like((tokens, ff)), like((ff, tokens)), like((d, tokens)), square, square),
        (tile_ff, tile_ff, tile_ff, across(ff, TILE), across(d, TILE), whole((d, ff)), whole((d, ff))),
        (), comm, number, 4 * tokens * d * ff, polls=2,
    )


def turn(h, p, wd, wg, wu, by_h, wd_last, number):
    tokens, d = h.shape
    ff = wg.shape[2]
    piece = ff // 3

    def body(step, ins, outs, scratch, poll):
        h_ref, p_ref, wd_ref, wg_ref, wu_ref, by_ref, last_ref = ins
        by_gate_ref, by_up_ref, pt_ref, at_ref, wg_out, wu_out, h_out = outs

        @pl.when(step == 0)
        def _():
            close_up(wg_ref, wg_out)
            close_up(wu_ref, wu_out)

        h = h_ref[...] + dot(p_ref[...], wd_ref[...], 1, 0).astype(BF16)
        h_out[...] = h
        a = normed(h)
        at_ref[...] = a.T
        by_h = by_ref[...]
        for c in range(3):
            part = pl.ds(piece * c, piece)
            gate = dot(a, wg_out[:, part], 1, 0)
            up = dot(a, wu_out[:, part], 1, 0)
            by_p = dot(by_h, last_ref[part, :], 1, 1).astype(BF16).astype(F32)
            pt_ref[part, :] = (gate * jax.nn.sigmoid(gate) * up).astype(BF16).T
            by_gate_ref[:, part], by_up_ref[:, part] = gated(by_p, gate, up)

    tile_d, tile_ff, square = over(TILE, d), over(TILE, ff), like((d, ff))
    return call(
        body, f"turn_{number}", tokens // TILE,
        (h, p, wd, wg, wu, by_h, wd_last),
        (tile_d, tile_ff, whole(wd.shape), whole(wg.shape), whole(wu.shape), tile_d, whole(wd.shape)),
        (like((tokens, ff)), like((tokens, ff)), like((ff, tokens)), like((d, tokens)), square, square, like(h.shape)),
        (tile_ff, tile_ff, across(ff, TILE), across(d, TILE), whole((d, ff)), whole((d, ff)), tile_d),
        (), NONE, number, 8 * tokens * d * ff,
    )[0]


def backward(by_h, later, earlier, comm, number):
    tokens, d = by_h.shape
    tile_d = over(TILE, d)
    ff = (later[1] if later else earlier[0]).shape[1]
    tile_ff = over(TILE, ff)
    piece = ff // 3

    def body(step, ins, outs, scratch, poll):
        by_ref, *ins = ins
        outs = list(outs)
        by_h = by_ref[...]
        poll()
        if later:
            h_ref, by_gate_ref, by_up_ref, wg_ref, wu_ref = ins[:5]
            by_a = dot(by_gate_ref[...], wg_ref[...], 1, 1).astype(BF16)
            by_a = (by_a + dot(by_up_ref[...], wu_ref[...], 1, 1).astype(BF16)).astype(F32)
            poll()
            wide = h_ref[...].astype(F32)
            scale = lax.rsqrt(jnp.mean(wide**2, -1, keepdims=True) + EPS)
            inner = jnp.mean(by_a * wide, -1, keepdims=True)
            by_h = by_h + (scale * (by_a - wide * (scale * scale * inner))).astype(BF16)
            outs.pop(0)[...] = by_h
        if earlier:
            gate_ref, up_ref, wd_ref = ins[-3:]
            for c in range(3):
                part = pl.ds(piece * c, piece)
                by_p = dot(by_h, wd_ref[part, :], 1, 1).astype(BF16).astype(F32)
                by_gate, by_up = gated(by_p, gate_ref[:, part], up_ref[:, part])
                outs[0][:, part] = by_gate
                outs[1][:, part] = by_up
            poll()

    ins, in_specs, outs, out_specs, polls = [by_h], [tile_d], [], [], 1
    if later:
        ins += later
        in_specs += [tile_d, tile_ff, tile_ff, whole((d, ff)), whole((d, ff))]
        outs.append(like((tokens, d)))
        out_specs.append(tile_d)
        polls += 1
    if earlier:
        ins += earlier
        in_specs += [tile_ff, tile_ff, whole((ff, d))]
        outs += [like((tokens, ff))] * 2
        out_specs += [tile_ff] * 2
        polls += 1
    flops = (4 * bool(later) + 2 * bool(earlier)) * tokens * d * ff
    return call(body, f"backward_{number}", tokens // TILE, ins, in_specs, outs, out_specs, (), comm, number, flops, polls)


def weight_terms(at, pt, by_gate, by_up, by_h, rows, number):
    d, tokens = at.shape
    ff = pt.shape[0]
    n = d // rows

    def body(step, ins, outs, scratch, poll):
        at_ref, pt_ref, by_gate_ref, by_up_ref, by_h_ref = ins
        wg_ref, wu_ref, wd_ref = outs
        for by_ref, w_ref in ((by_gate_ref, wg_ref), (by_up_ref, wu_ref)):
            term = dot(at_ref[...], by_ref[...], 1, 0)
            for j in range(n):
                w_ref[j] = term[rows * j : rows * j + rows].astype(BF16)
        wd_ref[...] = dot(pt_ref[...], by_h_ref[...], 1, 0).astype(BF16)

    blocks = pl.BlockSpec((n, rows, TILE), lambda i: (0, 0, i))
    wg, wu, wd = call(
        body, f"weight_terms_{number}", ff // TILE,
        (at, pt, by_gate, by_up, by_h),
        (whole(at.shape), over(TILE, tokens), across(tokens, TILE), across(tokens, TILE), whole(by_h.shape)),
        (like((n, rows, ff)), like((n, rows, ff)), like((ff, d))),
        (blocks, blocks, over(TILE, d)),
        (), NONE, number, 6 * tokens * d * ff,
    )[0]
    return wg, wu, wd.reshape(n, ff // n, d)


def gather_first(blocks):
    def body(step, ins, outs, scratch, poll):
        poll()

    return call(body, "gather_first", 1, (), (), (), (), (), Comm("gather", blocks), 0, 0)[1]


def solution(mesh):
    def step(x, dy, w_gate, w_up, w_down):
        rows, ff = w_gate.shape[1:]
        d = w_down.shape[2]

        x, dy = x[0], dy[0]
        wg0, wu0 = gather_first((w_gate[0], w_up[0]))
        (gate0, up0, p0, pt0, at0, wg0, wu0), (wd0, wg1, wu1, wd1) = forward(
            x, wg0, wu0, Comm("gather", (w_down[0], w_gate[1], w_up[1], w_down[1])), 1
        )
        wd0, wd1 = wd0.reshape(ff, d), wd1.reshape(ff, d)
        by_gate1, by_up1, pt1, at1, wg1, wu1, h1 = turn(x, p0, wd0, wg1, wu1, dy, wd1, 2)
        terms = weight_terms(at1, pt1, by_gate1, by_up1, dy, rows, 3)
        (by_h, by_gate0, by_up0), (sum_g1, sum_u1, sum_d1) = backward(
            dy, (h1, by_gate1, by_up1, wg1, wu1), (gate0, up0, wd0), Comm("scatter", terms), 4
        )
        terms = weight_terms(at0, pt0, by_gate0, by_up0, by_h, rows, 5)
        (by_x,), (sum_g0, sum_u0, sum_d0) = backward(by_h, (x, by_gate0, by_up0, wg0, wu0), (), Comm("scatter", terms), 6)
        return by_x[None], jnp.stack([sum_g0, sum_g1]), jnp.stack([sum_u0, sum_u1]), jnp.stack([sum_d0, sum_d1])

    tokens, weights = P(("rep", "dp"), None, None), P(None, "dp", None)
    sums = P("rep", "dp", None)
    return jax.shard_map(
        step,
        mesh=mesh,
        in_specs=(tokens, tokens, weights, weights, weights),
        out_specs=(tokens, sums, sums, sums),
        check_vma=False,
    )
```

time: 520 us -> 463 us (0.89)
  Pallas kernels: 503 us -> 446 us
    pallas_call x8 -> x7, Pallas kernels: 503 us -> 446 us  [call(): pl.pallas_call(kernel, grid=(grid,), out_shape=[*outs, *comm.shapes], in_...]
where the time goes in v3:
time: 463 us; the launch traced here: 462 us
  Pallas kernels  446 us (96%)
  local copies, waits for them, and re-layouts  12.4 us (3%)
    pallas_call x7, Pallas kernels, call(): pl.pallas_call(kernel, grid=(grid,), out_shape=[*outs, *comm.shapes], in_...  446 us

profile of v3, /device:TPU:0, one launch (start us, length us, event | category | flops | bytes accessed | tf_op | source)
XLA Modules:
  0.0 462.4 jit_solution(14583362468087499492)
XLA Ops:
  0.6 1.7 slice_bitcast_fusion
  2.3 1.5 fusion.1
  3.9 0.8 copy_bitcast_fusion.1
  4.6 1.5 fusion
  6.1 0.8 copy_bitcast_fusion
  6.9 54.5 %gather_first.1 = (bf16[32,28,2304]{2,1,0:T(8,128)(2,1)}, bf16[32,28,2304]{2,1,0:T(8,128)(2,1)}) custom-call(bf16[28,2304]{1,0:T(8,128)(2,1)} %get-tuple-element.87.refs_0_, bf16[28,2304]{1,0:T(8,128)(2,1)} %get-tuple-element.89.refs_1_), custom_call_target="tpu_custom_call" | custom-call | bytes 50000000 | tf_op jit(solution)/shard_map/gather_first/pallas_call | solution.py:278
  61.4 107.5 %forward_1.1 = (f32[2048,2304]{1,0:T(8,128)}, f32[2048,2304]{1,0:T(8,128)}, bf16[2048,2304]{1,0:T(8,128)(2,1)}, bf16[2304,2048]{1,0:T(8,128)(2,1)}, bf16[896,204...) custom-call(bf16[2048,896]{1,0:T(8,128)(2,1)} %bitcast.35, ...), custom_call_target="tpu_custom_call" | custom-call | flops 16911433728 | bytes 50000000 | tf_op jit(solution)/shard_map/forward_1/pallas_call | solution.py:278
  168.9 57.8 %turn_2.1 = (bf16[2048,2304]{1,0:T(8,128)(2,1)}, bf16[2048,2304]{1,0:T(8,128)(2,1)}, bf16[2304,2048]{1,0:T(8,128)(2,1)}, bf16[896,2048]{1,0:T(8,128)(2,1)}, bf16...) custom-call(bf16[2048,896]{1,0:T(8,128)(2,1)} %bitcast.36, ...), custom_call_target="tpu_custom_call" | custom-call | flops 33822867456 | bytes 50000000 | tf_op jit(solution)/shard_map/turn_2/pallas_call | solution.py:278
  226.7 33.8 %weight_terms_3.1 = (bf16[32,28,2304]{2,1,0:T(8,128)(2,1)}, bf16[32,28,2304]{2,1,0:T(8,128)(2,1)}, bf16[2304,896]{1,0:T(8,128)(2,1)}) custom-call(bf16[896,2048]{1,0:T(8,128)(2,1)} %get-tuple-element.54.refs_0_, bf16[2304,2048]{1,0:T(8,128)(2,1)} %get-tuple-element.55.refs_1_, bf16[2048,2304]{1,0:T(8,128)(2,1)} %get-tuple-element.48.refs_2_, ...), custom_call_target="tpu_custom_call" | custom-call | flops 25367150592 | bytes 50000000 | tf_op jit(solution)/shard_map/weight_terms_3/pallas_call | solution.py:278
  260.6 81.9 %backward_4.1 = (bf16[2048,896]{1,0:T(8,128)(2,1)}, bf16[2048,2304]{1,0:T(8,128)(2,1)}, bf16[2048,2304]{1,0:T(8,128)(2,1)}, bf16[28,2304]{1,0:T(8,128)(2,1)}, bf...) custom-call(bf16[2048,896]{1,0:T(8,128)(2,1)} %bitcast.34, bf16[2048,896]{1,0:T(8,128)(2,1)} %get-tuple-element.47.refs_1_, ...), custom_call_target="tpu_custom_call" | custom-call | flops 25367150592 | bytes 50000000 | tf_op jit(solution)/shard_map/backward_4/pallas_call | solution.py:278
  342.4 33.9 %weight_terms_5.1 = (bf16[32,28,2304]{2,1,0:T(8,128)(2,1)}, bf16[32,28,2304]{2,1,0:T(8,128)(2,1)}, bf16[2304,896]{1,0:T(8,128)(2,1)}) custom-call(bf16[896,2048]{1,0:T(8,128)(2,1)} %get-tuple-element.64.refs_0_, bf16[2304,2048]{1,0:T(8,128)(2,1)} %get-tuple-element.65.refs_1_, bf16[2048,2304]{1,0:T(8,128)(2,1)} %get-tuple-element.60.refs_2_, ...), custom_call_target="tpu_custom_call" | custom-call | flops 25367150592 | bytes 50000000 | tf_op jit(solution)/shard_map/weight_terms_5/pallas_call | solution.py:278
  376.3 0.0 copy-start.1
  376.3 0.0 copy-start.2
  376.3 0.0 copy-start
  376.3 76.4 %backward_6.1 = (bf16[2048,896]{1,0:T(8,128)(2,1)}, bf16[28,2304]{1,0:T(8,128)(2,1)}, bf16[28,2304]{1,0:T(8,128)(2,1)}, bf16[72,896]{1,0:T(8,128)(2,1)}) custom-call(bf16[2048,896]{1,0:T(8,128)(2,1)} %get-tuple-element.59.refs_4_.refs_0_, bf16[2048,896]{1,0:T(8,128)(2,1)} %bitcast.37, bf16[2048,2304]{1,0:T(8,128)(2,1)} %get-tuple-element.60.refs_2_, ...), custom_call_target="tpu_custom_call" | custom-call | flops 16911433728 | bytes 50000000 | tf_op jit(solution)/shard_map/backward_6/pallas_call | solution.py:278
  452.7 0.0 copy-done.1
  452.7 0.9 pad_maximum_fusion
  453.7 1.0 copy.13
  454.6 0.0 copy-done.2
  454.7 1.6 pad_maximum_fusion.2
  456.3 0.0 copy-done
  456.3 0.9 pad_maximum_fusion.1
  457.2 1.0 copy.14
  458.2 4.2 copy.24
Async XLA Ops:
  376.3 76.5 %copy-start.1 = (bf16[28,2304]{1,0:T(8,128)(2,1)S(1)}, bf16[28,2304]{1,0:T(8,128)(2,1)}, u32[]{:S(2)}) copy-start(bf16[28,2304]{1,0:T(8,128)(2,1)} %get-tuple-element.71) | copy-start | bytes 387076
  376.3 78.4 %copy-start.2 = (bf16[72,896]{1,0:T(8,128)(2,1)S(1)}, bf16[72,896]{1,0:T(8,128)(2,1)}, u32[]{:S(2)}) copy-start(bf16[72,896]{1,0:T(8,128)(2,1)} %get-tuple-element.75) | copy-start | bytes 387076
  376.3 80.0 %copy-start = (bf16[28,2304]{1,0:T(8,128)(2,1)S(1)}, bf16[28,2304]{1,0:T(8,128)(2,1)}, u32[]{:S(2)}) copy-start(bf16[28,2304]{1,0:T(8,128)(2,1)} %get-tuple-element.73) | copy-start | bytes 387076

commit v4 on v3

--- a/solution.py
+++ b/solution.py
@@ -188,7 +188,7 @@
         pltpu.make_async_copy(some, some, self.send).wait()
 
 
-PARTS = 2
+PARTS = 3
 
 
 def cuts(columns):

time: 463 us -> 467 us (level)
  no operation moved by 1% of the time
where the time goes in v4:
time: 467 us
  Pallas kernels  450 us (96%)
  local copies, waits for them, and re-layouts  12.4 us (3%)
    pallas_call x7, Pallas kernels, call(): pl.pallas_call(kernel, grid=(grid,), out_shape=[*outs, *comm.shapes], in_...  450 us

profile of v4, /device:TPU:0, one launch (start us, length us, event | category | flops | bytes accessed | tf_op | source)
XLA Modules:
  0.0 466.6 jit_solution(6721172502376501574)
XLA Ops:
  0.6 1.7 slice_bitcast_fusion
  2.3 1.5 fusion.1
  3.9 0.8 copy_bitcast_fusion.1
  4.6 1.5 fusion
  6.1 0.8 copy_bitcast_fusion
  6.9 54.5 %gather_first.1 = (bf16[32,28,2304]{2,1,0:T(8,128)(2,1)}, bf16[32,28,2304]{2,1,0:T(8,128)(2,1)}) custom-call(bf16[28,2304]{1,0:T(8,128)(2,1)} %get-tuple-element.87.refs_0_, bf16[28,2304]{1,0:T(8,128)(2,1)} %get-tuple-element.89.refs_1_), custom_call_target="tpu_custom_call" | custom-call | bytes 50000000 | tf_op jit(solution)/shard_map/gather_first/pallas_call | solution.py:278
  61.4 107.5 %forward_1.1 = (f32[2048,2304]{1,0:T(8,128)}, f32[2048,2304]{1,0:T(8,128)}, bf16[2048,2304]{1,0:T(8,128)(2,1)}, bf16[2304,2048]{1,0:T(8,128)(2,1)}, bf16[896,204...) custom-call(bf16[2048,896]{1,0:T(8,128)(2,1)} %bitcast.35, ...), custom_call_target="tpu_custom_call" | custom-call | flops 16911433728 | bytes 50000000 | tf_op jit(solution)/shard_map/forward_1/pallas_call | solution.py:278
  168.9 57.8 %turn_2.1 = (bf16[2048,2304]{1,0:T(8,128)(2,1)}, bf16[2048,2304]{1,0:T(8,128)(2,1)}, bf16[2304,2048]{1,0:T(8,128)(2,1)}, bf16[896,2048]{1,0:T(8,128)(2,1)}, bf16...) custom-call(bf16[2048,896]{1,0:T(8,128)(2,1)} %bitcast.36, ...), custom_call_target="tpu_custom_call" | custom-call | flops 33822867456 | bytes 50000000 | tf_op jit(solution)/shard_map/turn_2/pallas_call | solution.py:278
  226.7 33.8 %weight_terms_3.1 = (bf16[32,28,2304]{2,1,0:T(8,128)(2,1)}, bf16[32,28,2304]{2,1,0:T(8,128)(2,1)}, bf16[2304,896]{1,0:T(8,128)(2,1)}) custom-call(bf16[896,2048]{1,0:T(8,128)(2,1)} %get-tuple-element.54.refs_0_, bf16[2304,2048]{1,0:T(8,128)(2,1)} %get-tuple-element.55.refs_1_, bf16[2048,2304]{1,0:T(8,128)(2,1)} %get-tuple-element.48.refs_2_, ...), custom_call_target="tpu_custom_call" | custom-call | flops 25367150592 | bytes 50000000 | tf_op jit(solution)/shard_map/weight_terms_3/pallas_call | solution.py:278
  260.6 85.6 %backward_4.1 = (bf16[2048,896]{1,0:T(8,128)(2,1)}, bf16[2048,2304]{1,0:T(8,128)(2,1)}, bf16[2048,2304]{1,0:T(8,128)(2,1)}, bf16[28,2304]{1,0:T(8,128)(2,1)}, bf...) custom-call(bf16[2048,896]{1,0:T(8,128)(2,1)} %bitcast.34, bf16[2048,896]{1,0:T(8,128)(2,1)} %get-tuple-element.47.refs_1_, ...), custom_call_target="tpu_custom_call" | custom-call | flops 25367150592 | bytes 50000000 | tf_op jit(solution)/shard_map/backward_4/pallas_call | solution.py:278
  346.2 33.9 %weight_terms_5.1 = (bf16[32,28,2304]{2,1,0:T(8,128)(2,1)}, bf16[32,28,2304]{2,1,0:T(8,128)(2,1)}, bf16[2304,896]{1,0:T(8,128)(2,1)}) custom-call(bf16[896,2048]{1,0:T(8,128)(2,1)} %get-tuple-element.64.refs_0_, bf16[2304,2048]{1,0:T(8,128)(2,1)} %get-tuple-element.65.refs_1_, bf16[2048,2304]{1,0:T(8,128)(2,1)} %get-tuple-element.60.refs_2_, ...), custom_call_target="tpu_custom_call" | custom-call | flops 25367150592 | bytes 50000000 | tf_op jit(solution)/shard_map/weight_terms_5/pallas_call | solution.py:278
  380.1 0.0 copy-start.1
  380.1 0.0 copy-start.2
  380.1 0.0 copy-start
  380.1 76.9 %backward_6.1 = (bf16[2048,896]{1,0:T(8,128)(2,1)}, bf16[28,2304]{1,0:T(8,128)(2,1)}, bf16[28,2304]{1,0:T(8,128)(2,1)}, bf16[72,896]{1,0:T(8,128)(2,1)}) custom-call(bf16[2048,896]{1,0:T(8,128)(2,1)} %get-tuple-element.59.refs_4_.refs_0_, bf16[2048,896]{1,0:T(8,128)(2,1)} %bitcast.37, bf16[2048,2304]{1,0:T(8,128)(2,1)} %get-tuple-element.60.refs_2_, ...), custom_call_target="tpu_custom_call" | custom-call | flops 16911433728 | bytes 50000000 | tf_op jit(solution)/shard_map/backward_6/pallas_call | solution.py:278
  457.0 0.0 copy-done.1
  457.0 0.9 pad_maximum_fusion
  458.0 1.0 copy.13
  458.9 0.0 copy-done.2
  458.9 1.6 pad_maximum_fusion.2
  460.6 0.0 copy-done
  460.6 0.9 pad_maximum_fusion.1
  461.5 1.0 copy.14
  462.5 4.2 copy.24
Async XLA Ops:
  380.1 76.9 %copy-start.1 = (bf16[28,2304]{1,0:T(8,128)(2,1)S(1)}, bf16[28,2304]{1,0:T(8,128)(2,1)}, u32[]{:S(2)}) copy-start(bf16[28,2304]{1,0:T(8,128)(2,1)} %get-tuple-element.71) | copy-start | bytes 387076
  380.1 78.9 %copy-start.2 = (bf16[72,896]{1,0:T(8,128)(2,1)S(1)}, bf16[72,896]{1,0:T(8,128)(2,1)}, u32[]{:S(2)}) copy-start(bf16[72,896]{1,0:T(8,128)(2,1)} %get-tuple-element.75) | copy-start | bytes 387076
  380.1 80.5 %copy-start = (bf16[28,2304]{1,0:T(8,128)(2,1)S(1)}, bf16[28,2304]{1,0:T(8,128)(2,1)}, u32[]{:S(2)}) copy-start(bf16[28,2304]{1,0:T(8,128)(2,1)} %get-tuple-element.73) | copy-start | bytes 387076
